TPU v7x, 8 devices: a whole 2x2x1 slice. The times are simulated.
8 devices in a mesh: rep: 1 (over z), mp: 2 (over y), tok: 4 (over x, core).
Axes of the slice: x: 2, y: 2, z: 1, core: 2. Of those that a mesh axis runs over, the one named last changes fastest.
Arguments:
- hidden_in: bfloat16 [16384, 768], P(('rep', 'tok', 'mp'))
- seg_ids: int32 [16384], P(('rep', 'tok', 'mp'))
- expert_ids: int32 [16384, 2], P(('rep', 'tok', 'mp'))
- expert_gates: float32 [16384, 2], P(('rep', 'tok', 'mp'))
- w_query: bfloat16 [2, 768, 12, 64], P(None, 'tok', 'mp')
- w_key: bfloat16 [2, 768, 12, 64], P(None, 'tok', 'mp')
- w_value: bfloat16 [2, 768, 12, 64], P(None, 'tok', 'mp')
- w_out: bfloat16 [2, 12, 64, 768], P(None, 'mp', None, 'tok')
- w_gate: bfloat16 [2, 8, 768, 3072], P(None, None, 'tok', 'mp')
- w_up: bfloat16 [2, 8, 768, 3072], P(None, None, 'tok', 'mp')
- w_down: bfloat16 [2, 8, 3072, 768], P(None, None, 'mp', 'tok')
- gain_attn: bfloat16 [2, 768], replicated
- gain_mlp: bfloat16 [2, 768], replicated
Outputs:
- output: float32 [16384, 768], P(('rep', 'tok', 'mp'))
All inputs are finite; a program needn't handle non-finite values.
Results may differ from a plain program's by a relative error of at most 0.0101443.
Values are sent between devices in bfloat16 or wider.
A program may use at most 1 GiB of HBM per device.

v0:
```python
import jax
import jax.numpy as jnp
from jax import lax
from jax.sharding import PartitionSpec as P

EPS = 1e-5
ROPE_BASE = 10000.0


def rms_norm(residual, gain):
    inv_rms = lax.rsqrt(jnp.mean(residual * residual, axis=-1, keepdims=True) + EPS)
    return (residual * inv_rms * gain.astype(jnp.float32)).astype(jnp.bfloat16)


def request_positions(seg_rows):
    token_index = jnp.arange(seg_rows.shape[-1], dtype=jnp.int32)
    is_start = jnp.concatenate([jnp.ones(seg_rows.shape[:-1] + (1,), dtype=jnp.bool_), seg_rows[..., 1:] != seg_rows[..., :-1]], axis=-1)
    start_index = lax.cummax(jnp.where(is_start, token_index, 0), axis=seg_rows.ndim - 1)
    return token_index - start_index


def rope_tables(positions, head_dim):
    inv_freq = jnp.power(ROPE_BASE, -jnp.arange(head_dim // 2, dtype=jnp.float32) * 2.0 / head_dim)
    angles = positions.astype(jnp.float32)[..., None] * inv_freq
    return jnp.cos(angles)[..., None, :], jnp.sin(angles)[..., None, :]


def apply_rope(vectors, cosines, sines):
    half_dim = vectors.shape[-1] // 2
    first_half = vectors[..., :half_dim]
    second_half = vectors[..., half_dim:]
    return jnp.concatenate([first_half * cosines - second_half * sines, second_half * cosines + first_half * sines], axis=-1)


def block_attention(q_rot, k_rot, v_all, seg_query, query_index, seg_keys, key_index):
    n_query, kv_heads, groups, head_dim = q_rot.shape
    block = min(n_query, 512)
    num_blocks = n_query // block
    scale = head_dim ** -0.5

    def one_block(block_in):
        q_block, seg_block, index_block = block_in
        scores = jnp.einsum('bhgd,shd->hgbs', q_block, k_rot, preferred_element_type=jnp.float32) * scale
        allowed = (seg_block[:, None] == seg_keys[None, :]) & (key_index[None, :] <= index_block[:, None])
        attn_prob = jax.nn.softmax(jnp.where(allowed, scores, -1e30), axis=-1).astype(jnp.bfloat16)
        return jnp.einsum('hgbs,shd->bhgd', attn_prob, v_all, preferred_element_type=jnp.float32).astype(jnp.bfloat16)

    block_outs = lax.map(one_block, (q_rot.reshape(num_blocks, block, kv_heads, groups, head_dim), seg_query.reshape(num_blocks, block), query_index.reshape(num_blocks, block)))
    return block_outs.reshape(n_query, kv_heads * groups, head_dim)


def expert_mix(normed, pair_token, pair_gate, group_sizes, gate_weight, up_weight, down_weight):
    pair_rows = normed[pair_token]
    gate_pre = lax.ragged_dot(pair_rows, gate_weight, group_sizes, preferred_element_type=jnp.float32)
    up_pre = lax.ragged_dot(pair_rows, up_weight, group_sizes, preferred_element_type=jnp.float32)
    hidden_act = (jax.nn.silu(gate_pre) * up_pre).astype(jnp.bfloat16)
    down_out = lax.ragged_dot(hidden_act, down_weight, group_sizes, preferred_element_type=jnp.float32)
    return jax.ops.segment_sum(down_out * pair_gate[:, None], pair_token, num_segments=normed.shape[0])


def solution(mesh):
    token_spec = P(('rep', 'tok', 'mp'))
    row_spec = P(('rep', 'tok', 'mp'), None)
    head_weight = P(None, 'tok', 'mp', None)
    in_specs = (row_spec, token_spec, row_spec, row_spec, head_weight, head_weight, head_weight, P(None, 'mp', None, 'tok'), P(None, None, 'tok', 'mp'), P(None, None, 'tok', 'mp'), P(None, None, 'mp', 'tok'), P(None, None), P(None, None))

    def device_step(hidden_in, seg_ids, expert_ids, expert_gates, w_query, w_key, w_value, w_out, w_gate, w_up, w_down, gain_attn, gain_mlp):
        num_layers, _, q_local, head_dim = w_query.shape
        kv_local = w_key.shape[2]
        groups = q_local // kv_local
        num_experts = w_gate.shape[1]
        seg_full = lax.all_gather(seg_ids, 'mp', axis=0, tiled=True)
        ids_full = lax.all_gather(expert_ids, 'mp', axis=0, tiled=True)
        gates_full = lax.all_gather(expert_gates, 'mp', axis=0, tiled=True)
        seq_len = seg_full.shape[0]
        token_index = jnp.arange(seq_len, dtype=jnp.int32)
        cosines, sines = rope_tables(request_positions(seg_full), head_dim)
        flat_ids = ids_full.reshape(2 * seq_len)
        pair_order = jnp.argsort(flat_ids, stable=True)
        group_sizes = jnp.bincount(flat_ids, length=num_experts).astype(jnp.int32)
        pair_token = pair_order // 2
        pair_gate = gates_full.reshape(2 * seq_len)[pair_order]
        residual = hidden_in.astype(jnp.float32)
        for layer in range(num_layers):
            q_weight = lax.all_gather(w_query[layer], 'tok', axis=0, tiled=True)
            k_weight = lax.all_gather(w_key[layer], 'tok', axis=0, tiled=True)
            v_weight = lax.all_gather(w_value[layer], 'tok', axis=0, tiled=True)
            o_weight = lax.all_gather(w_out[layer], 'tok', axis=2, tiled=True)
            gate_weight = lax.all_gather(w_gate[layer], 'tok', axis=1, tiled=True)
            up_weight = lax.all_gather(w_up[layer], 'tok', axis=1, tiled=True)
            down_weight = lax.all_gather(w_down[layer], 'tok', axis=2, tiled=True)
            normed = lax.all_gather(rms_norm(residual, gain_attn[layer]), 'mp', axis=0, tiled=True)
            q_proj = jnp.einsum('se,ehd->shd', normed, q_weight, preferred_element_type=jnp.float32)
            k_proj = jnp.einsum('se,ehd->shd', normed, k_weight, preferred_element_type=jnp.float32)
            v_proj = jnp.einsum('se,ehd->shd', normed, v_weight, preferred_element_type=jnp.float32)
            q_rot = apply_rope(q_proj, cosines, sines).astype(jnp.bfloat16).reshape(seq_len, kv_local, groups, head_dim)
            k_rot = apply_rope(k_proj, cosines, sines).astype(jnp.bfloat16)
            attn_out = block_attention(q_rot, k_rot, v_proj.astype(jnp.bfloat16), seg_full, token_index, seg_full, token_index)
            attn_part = jnp.einsum('shd,hde->se', attn_out, o_weight, preferred_element_type=jnp.float32)
            residual = residual + lax.psum_scatter(attn_part, 'mp', scatter_dimension=0, tiled=True)
            normed = lax.all_gather(rms_norm(residual, gain_mlp[layer]), 'mp', axis=0, tiled=True)
            mix_part = expert_mix(normed, pair_token, pair_gate, group_sizes, gate_weight, up_weight, down_weight)
            residual = residual + lax.psum_scatter(mix_part, 'mp', scatter_dimension=0, tiled=True)
        return residual

    return jax.shard_map(device_step, mesh=mesh, in_specs=in_specs, out_specs=row_spec, check_vma=False)
```

profile of v0, /device:TPU:0, one launch (start us, length us, event | category | flops | bytes accessed | tf_op | source)
XLA Modules:
  0.0 3039.8 jit_solution(2868866219499906249)
XLA Ops:
  130.4 553.0 %while.22 = (s32[]{:T(128)}, bf16[8,512,6,1,64]{1,4,2,3,0:T(8,128)(2,1)}, s32[8,512]{1,0:T(8,128)S(1)}, s32[4096]{0:T(1024)S(1)}, s32[8,512]{1,0:T(8,128)S(1)}, ...) while((s32[]{:T(128)}, ...), condition=%wide.region_6.7_spmd.clone, body=%wide.region_3.6_spmd.clone.sunk | while | flops 3378702336 | bytes 166552688 | solution.py:48
  155.5 22.7 fusion.116
  224.5 22.7 fusion.116
  362.6 22.7 fusion.116
  500.7 22.7 fusion.116
  638.7 22.7 fusion.116
  713.2 131.3 %reduce-scatter.5.cloned.1.call-done = f32[2048,768]{1,0:T(8,128)} async-done(((f32[4096,768]{1,0:T(8,128)}), f32[2048,768]{1,0:T(8,128)}) %reduce-scatter.5.cloned.1.call-update) | async-done | bytes 6291472 | tf_op jit(solution)/shard_map/reduce_scatter | solution.py:100
  877.0 57.5 %scatter_custom_fusion = s32[8]{0:T(128)} fusion(s32[8192]{0:T(1024)S(1)} %reshape.312, s32[8192]{0:T(1024)S(1)} %ne.20, s32[]{:T(128)} %copy.89), kind=kCustom, calls=%fused_computation.117 | custom fusion | flops 8192 | bytes 36 | tf_op jit(solution)/shard_map/scatter-add | solution.py:80
  949.9 45.5 %gather_fusion.1 = f32[8192]{0:T(1024)S(1)} fusion(f32[8192]{0:T(1024)S(1)} %reshape.280, s32[8192]{0:T(1024)S(1)} %get-tuple-element.237), kind=kCustom, calls=%fused_computation.1 | custom fusion | bytes 98304 | tf_op jit(solution)/shard_map/gather | solution.py:82
  995.5 24.2 copy.45
  1019.7 40.6 %gather_fusion = bf16[8192,768]{1,0:T(8,128)(2,1)} fusion(bf16[4096,768]{1,0:T(8,128)(2,1)} %all-gather.27.cloned.1.call-done, s32[8192]{0:T(1024)S(1)} %get-tuple-element.238), kind=kCustom, calls=%fused_computation | custom fusion | bytes 25198592 | tf_op jit(solution)/shard_map/gather | solution.py:53
  1060.4 52.8 %ragged-dot-none.5 = f32[8192,1536]{1,0:T(8,128)} custom-call(s32[1]{0:T(128)} %get-tuple-element.115, s32[9]{0:T(128)} %get-tuple-element.116, s32[39]{0:T(128)} %get-tuple-element.117, s32[39]{0:T(128)} %get-tuple-element.118, s32[1]{0:T(128)} %get-tuple-element.115, bf16[8192,768]{1,0:T(8,128)(2,1)} %gather_fusion, bf16[8,768,1536]{2,1,0:T(8,128)(2,1)} %bitcast.234), custom_call_target="tpu_custom_call" | custom-call | flops 19327352832 | bytes 81788960 | tf_op jit(solution)/shard_map/ragged_dot_general/ragged-dot-none
  1113.2 55.6 %all-gather.35.cloned.1.call-done = bf16[1,8,768,1536]{3,2,1,0:T(8,128)(2,1)} async-done(((bf16[1,8,192,1536]{3,2,1,0:T(8,128)(2,1)}), bf16[1,8,768,1536]{3,2,1,0:T(8,128)(2,1)}) %all-gather.35.cloned.1.call-update) | async-done | bytes 18874384 | tf_op jit(solution)/shard_map/all_gather | solution.py:90
  1168.8 52.4 %ragged-dot-none.4 = f32[8192,1536]{1,0:T(8,128)} custom-call(s32[1]{0:T(128)} %get-tuple-element.115, s32[9]{0:T(128)} %get-tuple-element.116, s32[39]{0:T(128)} %get-tuple-element.117, s32[39]{0:T(128)} %get-tuple-element.118, s32[1]{0:T(128)} %get-tuple-element.115, bf16[8192,768]{1,0:T(8,128)(2,1)} %gather_fusion, bf16[8,768,1536]{2,1,0:T(8,128)(2,1)} %bitcast.235), custom_call_target="tpu_custom_call" | custom-call | flops 19327352832 | bytes 81788960 | tf_op jit(solution)/shard_map/ragged_dot_general/ragged-dot-none
  1221.2 40.6 %multiply_convert_fusion.1 = bf16[8192,1536]{1,0:T(8,128)(2,1)} fusion(f32[8192,1536]{1,0:T(8,128)} %ragged-dot-none.4, f32[8192,1536]{1,0:T(8,128)} %ragged-dot-none.5), kind=kLoop, calls=%fused_computation.49 | loop fusion | flops 75497472 | bytes 125829120 | tf_op jit(solution)/shard_map/convert_element_type | solution.py:56
  1261.8 50.7 %ragged-dot-none.3 = f32[8192,768]{1,0:T(8,128)} custom-call(s32[1]{0:T(128)} %get-tuple-element.115, s32[9]{0:T(128)} %get-tuple-element.116, s32[39]{0:T(128)} %get-tuple-element.117, s32[39]{0:T(128)} %get-tuple-element.118, s32[1]{0:T(128)} %get-tuple-element.115, bf16[8192,1536]{1,0:T(8,128)(2,1)} %multiply_convert_fusion.1, bf16[8,1536,768]{2,1,0:T(8,128)(2,1)} %bitcast.233), custom_call_target="tpu_custom_call" | custom-call | flops 19327352832 | bytes 69206048 | tf_op jit(solution)/shard_map/ragged_dot_general/ragged-dot-none
  1312.6 63.3 %scatter_custom_fusion.1 = f32[4096,768]{1,0:T(8,128)} fusion(s32[8192]{0:T(1024)} %get-tuple-element.239, f32[8192,768]{1,0:T(8,128)} %ragged-dot-none.3, f32[8192]{0:T(1024)S(1)} %gather_fusion.1, f32[]{:T(128)} %constant.82.clone.1), kind=kCustom, calls=%fused_computation.52 | custom fusion | flops 12582912 | bytes 37782016 | tf_op jit(solution)/shard_map/scatter-add | solution.py:58
  1376.0 141.8 %reduce-scatter.7.cloned.1.call-done = f32[2048,768]{1,0:T(8,128)} async-done(((f32[4096,768]{1,0:T(8,128)}), f32[2048,768]{1,0:T(8,128)}) %reduce-scatter.7.cloned.1.call-update) | async-done | bytes 6291472 | tf_op jit(solution)/shard_map/reduce_scatter | solution.py:103
  1629.5 558.6 %while.23 = (s32[]{:T(128)}, bf16[8,512,6,1,64]{1,4,2,3,0:T(8,128)(2,1)}, s32[8,512]{1,0:T(8,128)}, s32[4096]{0:T(1024)S(1)}, s32[8,512]{1,0:T(8,128)}, /*index=...) while((s32[]{:T(128)}, ...), condition=%wide.region_17.18_spmd.clone, body=%wide.region_14.17_spmd.clone.sunk | while | flops 3378702336 | bytes 166552688 | solution.py:48
  1655.0 22.7 fusion.123
  2212.6 135.3 %reduce-scatter.9.cloned.1.call-done = f32[2048,768]{1,0:T(8,128)} async-done(((f32[4096,768]{1,0:T(8,128)}), f32[2048,768]{1,0:T(8,128)}) %reduce-scatter.9.cloned.1.call-update) | async-done | bytes 6291472 | tf_op jit(solution)/shard_map/reduce_scatter | solution.py:100
  2359.5 24.2 copy.59
  2383.7 52.8 %all-gather.31.cloned.1.call-done = bf16[4096,768]{1,0:T(8,128)(2,1)} async-done(((bf16[2048,768]{1,0:T(8,128)(2,1)}), bf16[4096,768]{1,0:T(8,128)(2,1)}) %all-gather.31.cloned.1.call-update) | async-done | bytes 6291472 | tf_op jit(solution)/shard_map/all_gather | solution.py:101
  2436.5 40.6 %gather_fusion.2 = bf16[8192,768]{1,0:T(8,128)(2,1)} fusion(bf16[4096,768]{1,0:T(8,128)(2,1)} %all-gather.31.cloned.1.call-done, s32[8192]{0:T(1024)S(1)} %copy-done.22), kind=kCustom, calls=%fused_computation.2 | custom fusion | bytes 25198592 | tf_op jit(solution)/shard_map/gather | solution.py:53
  2477.1 78.7 %all-gather.39.cloned.1.call-done = bf16[1,8,768,1536]{3,2,1,0:T(8,128)(2,1)} async-done(((bf16[1,8,192,1536]{3,2,1,0:T(8,128)(2,1)}), bf16[1,8,768,1536]{3,2,1,0:T(8,128)(2,1)}) %all-gather.39.cloned.1.call-update) | async-done | bytes 18874384 | tf_op jit(solution)/shard_map/all_gather | solution.py:89
  2555.8 52.5 %ragged-dot-none.2 = f32[8192,1536]{1,0:T(8,128)} custom-call(s32[1]{0:T(128)} %get-tuple-element.115, s32[9]{0:T(128)} %get-tuple-element.116, s32[39]{0:T(128)} %get-tuple-element.117, s32[39]{0:T(128)} %get-tuple-element.118, s32[1]{0:T(128)} %get-tuple-element.115, bf16[8192,768]{1,0:T(8,128)(2,1)} %gather_fusion.2, bf16[8,768,1536]{2,1,0:T(8,128)(2,1)} %bitcast.236), custom_call_target="tpu_custom_call" | custom-call | flops 19327352832 | bytes 81788960 | tf_op jit(solution)/shard_map/ragged_dot_general/ragged-dot-none
  2608.4 66.8 %all-gather.41.cloned.1.call-done = bf16[1,8,768,1536]{3,2,1,0:T(8,128)(2,1)} async-done(((bf16[1,8,192,1536]{3,2,1,0:T(8,128)(2,1)}), bf16[1,8,768,1536]{3,2,1,0:T(8,128)(2,1)}) %all-gather.41.cloned.1.call-update) | async-done | bytes 18874384 | tf_op jit(solution)/shard_map/all_gather | solution.py:90
  2675.2 52.4 %ragged-dot-none.1 = f32[8192,1536]{1,0:T(8,128)} custom-call(s32[1]{0:T(128)} %get-tuple-element.115, s32[9]{0:T(128)} %get-tuple-element.116, s32[39]{0:T(128)} %get-tuple-element.117, s32[39]{0:T(128)} %get-tuple-element.118, s32[1]{0:T(128)} %get-tuple-element.115, bf16[8192,768]{1,0:T(8,128)(2,1)} %gather_fusion.2, bf16[8,768,1536]{2,1,0:T(8,128)(2,1)} %bitcast.237), custom_call_target="tpu_custom_call" | custom-call | flops 19327352832 | bytes 81788960 | tf_op jit(solution)/shard_map/ragged_dot_general/ragged-dot-none
  2727.6 40.6 %multiply_convert_fusion = bf16[8192,1536]{1,0:T(8,128)(2,1)} fusion(f32[8192,1536]{1,0:T(8,128)} %ragged-dot-none.1, f32[8192,1536]{1,0:T(8,128)} %ragged-dot-none.2), kind=kLoop, calls=%fused_computation.48 | loop fusion | flops 75497472 | bytes 125829120 | tf_op jit(solution)/shard_map/convert_element_type | solution.py:56
  2768.2 50.8 %ragged-dot-none = f32[8192,768]{1,0:T(8,128)} custom-call(s32[1]{0:T(128)} %get-tuple-element.115, s32[9]{0:T(128)} %get-tuple-element.116, s32[39]{0:T(128)} %get-tuple-element.117, s32[39]{0:T(128)} %get-tuple-element.118, s32[1]{0:T(128)} %get-tuple-element.115, bf16[8192,1536]{1,0:T(8,128)(2,1)} %multiply_convert_fusion, bf16[8,1536,768]{2,1,0:T(8,128)(2,1)} %bitcast.232), custom_call_target="tpu_custom_call" | custom-call | flops 19327352832 | bytes 69206048 | tf_op jit(solution)/shard_map/ragged_dot_general/ragged-dot-none
  2818.9 63.3 %scatter_custom_fusion.2 = f32[4096,768]{1,0:T(8,128)} fusion(s32[8192]{0:T(1024)} %get-tuple-element.239, f32[8192,768]{1,0:T(8,128)} %ragged-dot-none, f32[8192]{0:T(1024)S(1)} %copy-done.20, f32[]{:T(128)} %constant.82.clone.1), kind=kCustom, calls=%fused_computation.50 | custom fusion | flops 12582912 | bytes 37782016 | tf_op jit(solution)/shard_map/scatter-add | solution.py:58
  2882.3 141.8 %reduce-scatter.11.cloned.1.call-done = f32[2048,768]{1,0:T(8,128)} async-done(((f32[4096,768]{1,0:T(8,128)}), f32[2048,768]{1,0:T(8,128)}) %reduce-scatter.11.cloned.1.call-update) | async-done | bytes 6291472 | tf_op jit(solution)/shard_map/reduce_scatter | solution.py:103
  (278 shorter events, 1330.3 us)
Async XLA Ops:
  7.4 100.2 %all-gather.25.cloned.1.call-start = ((), (), s32[]{:S(2)}) async-start(), calls=%async_computation.4 | async-start | bytes 9437184 | tf_op jit(solution)/shard_map/all_gather | solution.py:92
  8.7 13.4 copy-start.17
  11.4 30.3 copy-start.18
  15.8 828.6 %reduce-scatter.5.cloned.1.call-start = ((), (), s32[]{:S(2)}) async-start(), calls=%async_computation.5 | async-start | bytes 18874368 | tf_op jit(solution)/shard_map/reduce_scatter | solution.py:100
  107.6 7.9 copy-start.5
  107.6 7.9 copy-start.7
  683.9 7.1 copy-start.24
  701.2 294.4 %all-gather.37.cloned.1.call-start = ((), (), s32[]{:S(2)}) async-start(), calls=%async_computation.14 | async-start | bytes 23592960 | tf_op jit(solution)/shard_map/all_gather | solution.py:91
  707.7 136.7 %copy-start = (bf16[2048,768]{1,0:T(8,128)(2,1)S(1)}, bf16[2048,768]{1,0:T(8,128)(2,1)}, u32[]{:S(2)}) copy-start(bf16[2048,768]{1,0:T(8,128)(2,1)} %param.17) | copy-start | bytes 9437188
  712.5 307.2 %all-gather.27.cloned.1.call-start = ((), (), s32[]{:S(2)}) async-start(), calls=%async_computation.6 | async-start | bytes 9437184 | tf_op jit(solution)/shard_map/all_gather | solution.py:101
  851.3 209.0 %all-gather.33.cloned.1.call-start = ((), (), s32[]{:S(2)}) async-start(), calls=%async_computation.12 | async-start | bytes 23592960 | tf_op jit(solution)/shard_map/all_gather | solution.py:89
  859.7 8.5 copy-start.27
  859.8 309.1 %all-gather.35.cloned.1.call-start = ((), (), s32[]{:S(2)}) async-start(), calls=%async_computation.13 | async-start | bytes 23592960 | tf_op jit(solution)/shard_map/all_gather | solution.py:90
  868.2 68.1 %copy-start.28 = (f32[2048,2]{0,1:T(2,128)S(1)}, f32[2048,2]{0,1:T(2,128)}, u32[]{:S(2)}) copy-start(f32[2048,2]{0,1:T(2,128)} %param.20) | copy-start | bytes 49156
  868.2 649.6 %reduce-scatter.7.cloned.1.call-start = ((), (), s32[]{:S(2)}) async-start(), calls=%async_computation.7 | async-start | bytes 18874368 | tf_op jit(solution)/shard_map/reduce_scatter | solution.py:103
  949.9 69.8 %copy-start.21 = (s32[8192]{0:T(1024)}, s32[8192]{0:T(1024)S(1)}, u32[]{:S(2)}) copy-start(s32[8192]{0:T(1024)S(1)} %get-tuple-element.238) | copy-start | bytes 98308
  995.5 317.1 %copy-start.19 = (f32[8192]{0:T(1024)}, f32[8192]{0:T(1024)S(1)}, u32[]{:S(2)}) copy-start(f32[8192]{0:T(1024)S(1)} %gather_fusion.1) | copy-start | bytes 98308
  1375.9 141.8 %copy-start.1 = (bf16[2048,768]{1,0:T(8,128)(2,1)S(1)}, bf16[2048,768]{1,0:T(8,128)(2,1)}, u32[]{:S(2)}) copy-start(bf16[2048,768]{1,0:T(8,128)(2,1)} %param.17) | copy-start | bytes 9437188
  1375.9 150.2 %copy-start.25 = (f32[768]{0:T(1024)S(1)}, f32[768]{0:T(1024)}, u32[]{:S(2)}) copy-start(f32[768]{0:T(1024)} %get-tuple-element.165) | copy-start | bytes 9220
  1375.9 230.9 %all-gather.29.cloned.1.call-start = ((), (), s32[]{:S(2)}) async-start(), calls=%async_computation.8 | async-start | bytes 9437184 | tf_op jit(solution)/shard_map/all_gather | solution.py:92
  1528.5 19.1 copy-start.12
  1528.5 38.1 %copy-start.13 = (bf16[1,192,6,64]{1,3,2,0:T(8,128)(2,1)S(1)}, bf16[1,192,6,64]{1,3,2,0:T(8,128)(2,1)}, u32[]{:S(2)}) copy-start(bf16[1,192,6,64]{1,3,2,0:T(8,128)(2,1)} %get-tuple-element.231) | copy-start | bytes 442372
  1528.5 819.4 %reduce-scatter.9.cloned.1.call-start = ((), (), s32[]{:S(2)}) async-start(), calls=%async_computation.9 | async-start | bytes 18874368 | tf_op jit(solution)/shard_map/reduce_scatter | solution.py:100
  1546.0 40.1 %copy-start.14 = (bf16[1,6,64,192]{3,2,1,0:T(8,128)(2,1)S(1)}, bf16[1,6,64,192]{3,2,1,0:T(8,128)(2,1)}, u32[]{:S(2)}) copy-start(bf16[1,6,64,192]{3,2,1,0:T(8,128)(2,1)} %get-tuple-element.229) | copy-start | bytes 442372
  2205.4 154.1 %all-gather.43.cloned.1.call-start = ((), (), s32[]{:S(2)}) async-start(), calls=%async_computation.17 | async-start | bytes 23592960 | tf_op jit(solution)/shard_map/all_gather | solution.py:91
  2212.5 143.4 %copy-start.26 = (f32[768]{0:T(1024)S(1)}, f32[768]{0:T(1024)}, u32[]{:S(2)}) copy-start(f32[768]{0:T(1024)} %get-tuple-element.163) | copy-start | bytes 9220
  2212.5 224.0 %all-gather.31.cloned.1.call-start = ((), (), s32[]{:S(2)}) async-start(), calls=%async_computation.10 | async-start | bytes 9437184 | tf_op jit(solution)/shard_map/all_gather | solution.py:101
  2358.2 197.6 %all-gather.39.cloned.1.call-start = ((), (), s32[]{:S(2)}) async-start(), calls=%async_computation.15 | async-start | bytes 23592960 | tf_op jit(solution)/shard_map/all_gather | solution.py:89
  2358.8 316.4 %all-gather.41.cloned.1.call-start = ((), (), s32[]{:S(2)}) async-start(), calls=%async_computation.16 | async-start | bytes 23592960 | tf_op jit(solution)/shard_map/all_gather | solution.py:90
  2359.4 77.1 %copy-start.22 = (s32[8192]{0:T(1024)S(1)}, s32[8192]{0:T(1024)}, u32[]{:S(2)}) copy-start(s32[8192]{0:T(1024)} %copy-done.21) | copy-start | bytes 98308
  2359.4 664.7 %reduce-scatter.11.cloned.1.call-start = ((), (), s32[]{:S(2)}) async-start(), calls=%async_computation.11 | async-start | bytes 18874368 | tf_op jit(solution)/shard_map/reduce_scatter | solution.py:103
  2768.2 50.8 %copy-start.20 = (f32[8192]{0:T(1024)S(1)}, f32[8192]{0:T(1024)}, u32[]{:S(2)}) copy-start(f32[8192]{0:T(1024)} %copy-done.19) | copy-start | bytes 98308
  (15 other events, 61.7 us)
Sparse Core Ops, SparseCore 0:
  15.9 81.0 all-gather.24
  701.3 143.1 reduce-scatter.4
  1376.0 141.6 reduce-scatter.6
  1528.6 78.2 all-gather.28
  2205.5 142.3 reduce-scatter.8
  2882.4 141.6 reduce-scatter.10
Sparse Core Ops, SparseCore 1:
  712.6 119.4 all-gather.36
  851.4 78.5 all-gather.26
  931.4 117.9 all-gather.32
  1050.9 117.9 all-gather.34
  2212.6 118.7 all-gather.42
  2358.3 78.1 all-gather.30
  2437.9 117.9 all-gather.38
  2557.2 117.9 all-gather.40
where the time goes:
time: 3060 us; the launch traced here: 3040 us
  waiting for transfers between devices  806 us (26%)
  matrix products  739 us (24%)
  other arithmetic  735 us (24%)
  Pallas kernels  313 us (10%)
  local copies, waits for them, and re-layouts  269 us (9%)
  blocking collectives  159 us (5%)
    reduce_sum x16, other arithmetic, one_block(): jax.nn.softmax(jnp.where(allowed, scores, -1e+30), axis=-1)  362 us
    dot_general x16, matrix products, one_block(): jnp.einsum('bhgd,shd->hgbs', q_block, k_rot, preferred_element_type=jnp.f...  350 us
    dot_general x16, matrix products, one_block(): jnp.einsum('hgbs,shd->bhgd', attn_prob, v_all, preferred_element_type=jnp...  348 us
    another operation x6, Pallas kernels  312 us
    reduce_scatter x2, waiting for transfers between devices, device_step(): lax.psum_scatter(mix_part, 'mp', scatter_dimension=0, tiled=True)  284 us
    reduce_scatter x2, waiting for transfers between devices, device_step(): lax.psum_scatter(attn_part, 'mp', scatter_dimension=0, tiled=True)  267 us
    scatter-add x2, other arithmetic, expert_mix(): jax.ops.segment_sum(down_out * pair_gate[:, None], pair_token, num_segmen...  127 us
    all_gather x2, waiting for transfers between devices, device_step(): up_weight = lax.all_gather(w_up[layer], 'tok', axis=1, tiled=True)  122 us
  transfers between devices with their start and end apart: 14, of which 9 were waited for; matrix products, arithmetic and copies ran while one was open for 10% of the time, Pallas kernels for 4%

commit v1 on v0

v1 whole, which is shorter than its diff:
```python
import functools

import jax
import jax.numpy as jnp
from jax import lax
from jax.experimental import pallas as pl
from jax.experimental.pallas import tpu as pltpu
from jax.sharding import PartitionSpec as P

EPS = 1e-5
ROPE_BASE = 10000.0
BLOCK = 256
TILE = 256
BATCH = 16
MASKED = -1e30


def rms_norm(residual, gain):
    inv_rms = lax.rsqrt(jnp.mean(residual * residual, axis=-1, keepdims=True) + EPS)
    return (residual * inv_rms * gain.astype(jnp.float32)).astype(jnp.bfloat16)


def request_starts(seg_rows):
    token_index = jnp.arange(seg_rows.shape[0], dtype=jnp.int32)
    is_start = jnp.concatenate([jnp.ones((1,), dtype=jnp.bool_), seg_rows[1:] != seg_rows[:-1]])
    return lax.cummax(jnp.where(is_start, token_index, 0), axis=0)


def rope_tables(positions, head_dim):
    half = head_dim // 2
    lane = jnp.arange(2 * head_dim, dtype=jnp.int32)
    inv_freq = jnp.power(ROPE_BASE, -(lane % half).astype(jnp.float32) * 2.0 / head_dim)
    angles = positions.astype(jnp.float32)[:, None] * inv_freq[None, :]
    sign = jnp.where(lane % head_dim < half, -1.0, 1.0).astype(jnp.float32)
    return jnp.cos(angles), jnp.sin(angles) * sign


def attention_kernel(lo_ref, mid_ref, h_ref, cos_ref, sin_ref, pos_ref, w_ref, out_ref,
                     k_scr, v_scr, q_scr, m_scr, l_scr, acc_scr, *, pairs, head_dim):
    i = pl.program_id(0)
    width = 2 * head_dim
    span = pairs * width
    half = head_dim // 2
    lane = lax.broadcasted_iota(jnp.int32, (BLOCK, width), 1)
    low_half = lane % head_dim < half
    first_head = lane < head_dim
    cosines = cos_ref[...]
    sines = sin_ref[...]
    h_block = h_ref[...]
    row0 = pl.multiple_of(i * BLOCK, BLOCK)
    for p in range(pairs):
        cols = pl.ds(p * width, width)
        q = jnp.dot(h_block, w_ref[:, pl.ds(p * width, width)], preferred_element_type=jnp.float32)
        k = jnp.dot(h_block, w_ref[:, pl.ds(span + p * width, width)], preferred_element_type=jnp.float32)
        v = jnp.dot(h_block, w_ref[:, pl.ds(2 * span + p * width, width)], preferred_element_type=jnp.float32)
        q_turn = jnp.where(low_half, pltpu.roll(q, width - half, 1), pltpu.roll(q, half, 1))
        k_turn = jnp.where(low_half, pltpu.roll(k, width - half, 1), pltpu.roll(k, half, 1))
        q_rot = (q * cosines + q_turn * sines).astype(jnp.bfloat16).astype(jnp.float32) * (head_dim ** -0.5)
        k_rot = (k * cosines + k_turn * sines).astype(jnp.bfloat16)
        q_scr[2 * p] = jnp.where(first_head, q_rot, 0.0).astype(jnp.bfloat16)
        q_scr[2 * p + 1] = jnp.where(first_head, 0.0, q_rot).astype(jnp.bfloat16)
        k_scr[p, pl.ds(row0, BLOCK), :] = k_rot
        v_scr[p, pl.ds(2 * row0, BLOCK), :] = jnp.where(first_head, v, 0.0).astype(jnp.bfloat16)
        v_scr[p, pl.ds(2 * row0 + BLOCK, BLOCK), :] = jnp.where(first_head, 0.0, v).astype(jnp.bfloat16)

    m_scr[...] = jnp.full_like(m_scr, MASKED)
    l_scr[...] = jnp.zeros_like(l_scr)
    acc_scr[...] = jnp.zeros_like(acc_scr)

    def step(j, masked):
        col0 = pl.multiple_of(j * BLOCK, BLOCK)
        if masked:
            gap = (lax.broadcasted_iota(jnp.int32, (BLOCK, BLOCK), 0) - lax.broadcasted_iota(jnp.int32, (BLOCK, BLOCK), 1)) + (row0 - col0)
            allowed = (gap >= 0) & (gap <= pos_ref[...])
        for p in range(pairs):
            k_block = k_scr[p, pl.ds(col0, BLOCK), :]
            probs = []
            scales = []
            for e in range(2):
                hd = 2 * p + e
                s = lax.dot_general(q_scr[hd], k_block, (((1,), (1,)), ((), ())), preferred_element_type=jnp.float32)
                if masked:
                    s = jnp.where(allowed, s, MASKED)
                m_old = m_scr[hd]
                m_new = jnp.maximum(m_old, jnp.max(s, axis=1, keepdims=True))
                alpha = jnp.exp(m_old - m_new)
                m_wide = jnp.concatenate([m_new] * (BLOCK // width), axis=1)
                e_s = jnp.exp(s - m_wide)
                if masked:
                    e_s = jnp.where(allowed, e_s, 0.0)
                part = e_s[:, :width]
                for c in range(1, BLOCK // width):
                    part = part + e_s[:, c * width:(c + 1) * width]
                l_scr[hd] = l_scr[hd] * alpha + part
                m_scr[hd] = m_new
                probs.append(e_s.astype(jnp.bfloat16))
                scales.append(alpha)
            pv = jnp.dot(jnp.concatenate(probs, axis=1), v_scr[p, pl.ds(2 * col0, 2 * BLOCK), :], preferred_element_type=jnp.float32)
            acc_scr[p] = acc_scr[p] * jnp.where(first_head, scales[0], scales[1]) + pv

    def masked_step(j, carry):
        step(j, True)
        return carry

    def plain_step(j, carry):
        step(j, False)
        return carry

    lax.fori_loop(lo_ref[i], mid_ref[i], masked_step, 0)
    lax.fori_loop(mid_ref[i], i, plain_step, 0)
    step(i, True)

    outs = []
    for p in range(pairs):
        l0 = jnp.sum(l_scr[2 * p], axis=1, keepdims=True)
        l1 = jnp.sum(l_scr[2 * p + 1], axis=1, keepdims=True)
        outs.append((acc_scr[p] / jnp.where(first_head, l0, l1)).astype(jnp.bfloat16))
    o = jnp.concatenate(outs, axis=1)
    out_ref[...] = lax.dot_general(o, w_ref[:, pl.ds(3 * span, span)], (((1,), (1,)), ((), ())), preferred_element_type=jnp.float32)


def attention(normed, weight, cosines, sines, positions, lo, mid, heads, head_dim):
    seq, hidden = normed.shape
    pairs = heads // 2
    width = 2 * head_dim
    blocks = seq // BLOCK
    span = pairs * width
    flops = 2 * seq * hidden * 4 * span + 4 * seq * (seq // 4) * span
    return pl.pallas_call(
        functools.partial(attention_kernel, pairs=pairs, head_dim=head_dim),
        name='attn',
        out_shape=jax.ShapeDtypeStruct((seq, hidden), jnp.float32),
        grid_spec=pltpu.PrefetchScalarGridSpec(
            num_scalar_prefetch=2,
            grid=(blocks,),
            in_specs=[
                pl.BlockSpec((BLOCK, hidden), lambda i, *_: (i, 0)),
                pl.BlockSpec((BLOCK, width), lambda i, *_: (i, 0)),
                pl.BlockSpec((BLOCK, width), lambda i, *_: (i, 0)),
                pl.BlockSpec((BLOCK, 1), lambda i, *_: (i, 0)),
                pl.BlockSpec(weight.shape, lambda i, *_: (0, 0)),
            ],
            out_specs=pl.BlockSpec((BLOCK, hidden), lambda i, *_: (i, 0)),
            scratch_shapes=[
                pltpu.VMEM((pairs, seq, width), jnp.bfloat16),
                pltpu.VMEM((pairs, 2 * seq, width), jnp.bfloat16),
                pltpu.VMEM((heads, BLOCK, width), jnp.bfloat16),
                pltpu.VMEM((heads, BLOCK, width), jnp.float32),
                pltpu.VMEM((heads, BLOCK, width), jnp.float32),
                pltpu.VMEM((pairs, BLOCK, width), jnp.float32),
            ],
        ),
        compiler_params=pltpu.CompilerParams(dimension_semantics=('arbitrary',), vmem_limit_bytes=48 * 1024 * 1024),
        cost_estimate=pl.CostEstimate(flops=flops, bytes_accessed=6 * seq * hidden, transcendentals=seq * (seq // 4) * heads),
    )(lo, mid, normed, cosines, sines, positions, weight)


def moe_kernel(tile_start_ref, tok_ref, gate_ref, h_hbm, wg_ref, wu_ref, wd_ref, out_hbm,
               h_scr, acc_scr, x_scr, y_scr, a_scr, in_scr, out_scr, in_sem, out_sem, *, seq, hidden):
    e = pl.program_id(0)
    last = pl.num_programs(0) - 1
    groups = hidden // 128
    chunks = seq // TILE

    def fetch(c, slot):
        return pltpu.make_async_copy(h_hbm.at[pl.ds(pl.multiple_of(c * TILE, TILE), TILE), :], in_scr.at[slot], in_sem.at[slot])

    @pl.when(e == 0)
    def _():
        fetch(0, 0).start()

        def load(c, carry):
            slot = lax.rem(c, 2)

            @pl.when(c + 1 < chunks)
            def _():
                fetch(c + 1, 1 - slot).start()

            fetch(c, slot).wait()
            rows = in_scr[slot].astype(jnp.float32)
            for g in range(groups):
                h_scr[pl.ds(pl.multiple_of(c * TILE, TILE), TILE), g, :] = rows[:, g * 128:(g + 1) * 128]
            acc_scr[pl.ds(pl.multiple_of(c * TILE, TILE), TILE)] = jnp.zeros((TILE, 8, 128), jnp.float32)
            return carry

        lax.fori_loop(0, chunks, load, 0)
        h_scr[pl.ds(seq, 8)] = jnp.zeros((8, 8, 128), jnp.float32)

    w_gate = wg_ref[...].reshape(hidden, wg_ref.shape[-1])
    w_up = wu_ref[...].reshape(hidden, wu_ref.shape[-1])
    w_down = wd_ref[...].reshape(hidden, wd_ref.shape[-1])
    ffn = wg_ref.shape[-1]
    step_n = 512

    def tile_body(t, carry):
        base = t * TILE

        def gather(b, carry):
            first = base + b * BATCH
            vals = [h_scr[tok_ref[first + r]] for r in range(BATCH)]
            for r in range(BATCH):
                x_scr[b * BATCH + r] = vals[r]
            return carry

        lax.fori_loop(0, TILE // BATCH, gather, 0)
        x = jnp.concatenate([x_scr[:, g, :] for g in range(groups)], axis=1).astype(jnp.bfloat16)
        for n in range(0, ffn, step_n):
            gate_pre = jnp.dot(x, wg_ref[:, 0, :, pl.ds(n, step_n)].reshape(hidden, step_n), preferred_element_type=jnp.float32)
            up_pre = jnp.dot(x, wu_ref[:, 0, :, pl.ds(n, step_n)].reshape(hidden, step_n), preferred_element_type=jnp.float32)
            a_scr[:, pl.ds(n, step_n)] = (gate_pre * jax.nn.sigmoid(gate_pre) * up_pre).astype(jnp.bfloat16)
        y = lax.dot_general(a_scr[...], wd_ref[:, 0].reshape(hidden, ffn), (((1,), (1,)), ((), ())), preferred_element_type=jnp.float32)
        for g in range(groups):
            y_scr[:, g, :] = y[:, g * 128:(g + 1) * 128]

        def scatter(b, carry):
            first = base + b * BATCH
            toks = [tok_ref[first + r] for r in range(BATCH)]
            vals = [acc_scr[toks[r]] + gate_ref[first + r] * y_scr[b * BATCH + r] for r in range(BATCH)]
            for r in range(BATCH):
                acc_scr[toks[r]] = vals[r]
            return carry

        lax.fori_loop(0, TILE // BATCH, scatter, 0)
        return carry

    lax.fori_loop(tile_start_ref[e], tile_start_ref[e + 1], tile_body, 0)

    def flush(c, slot):
        return pltpu.make_async_copy(out_scr.at[slot], out_hbm.at[pl.ds(pl.multiple_of(c * TILE, TILE), TILE), :], out_sem.at[slot])

    @pl.when(e == last)
    def _():
        def store(c, carry):
            slot = lax.rem(c, 2)

            @pl.when(c >= 2)
            def _():
                flush(c - 2, slot).wait()

            for g in range(groups):
                out_scr[slot, :, pl.ds(g * 128, 128)] = acc_scr[pl.ds(pl.multiple_of(c * TILE, TILE), TILE), g, :]
            flush(c, slot).start()
            return carry

        lax.fori_loop(0, chunks, store, 0)
        flush(chunks - 2, lax.rem(chunks - 2, 2)).wait()
        flush(chunks - 1, lax.rem(chunks - 1, 2)).wait()


def expert_mix(normed, tile_start, pair_token, pair_gate, w_gate, w_up, w_down):
    seq, hidden = normed.shape
    parts, experts, depth, ffn = w_gate.shape
    weight_spec = pl.BlockSpec((parts, 1, depth, ffn), lambda e, *_: (0, e, 0, 0))
    return pl.pallas_call(
        functools.partial(moe_kernel, seq=seq, hidden=hidden),
        name='moe',
        out_shape=jax.ShapeDtypeStruct((seq, hidden), jnp.float32),
        grid_spec=pltpu.PrefetchScalarGridSpec(
            num_scalar_prefetch=3,
            grid=(experts,),
            in_specs=[pl.BlockSpec(memory_space=pl.ANY), weight_spec, weight_spec, weight_spec],
            out_specs=pl.BlockSpec(memory_space=pl.ANY),
            scratch_shapes=[
                pltpu.VMEM((seq + 8, 8, 128), jnp.float32),
                pltpu.VMEM((seq + 8, 8, 128), jnp.float32),
                pltpu.VMEM((TILE, 8, 128), jnp.float32),
                pltpu.VMEM((TILE, 8, 128), jnp.float32),
                pltpu.VMEM((TILE, ffn), jnp.bfloat16),
                pltpu.VMEM((2, TILE, hidden), jnp.bfloat16),
                pltpu.VMEM((2, TILE, hidden), jnp.float32),
                pltpu.SemaphoreType.DMA((2,)),
                pltpu.SemaphoreType.DMA((2,)),
            ],
        ),
        compiler_params=pltpu.CompilerParams(dimension_semantics=('arbitrary',), vmem_limit_bytes=63 * 1024 * 1024),
        cost_estimate=pl.CostEstimate(flops=2 * 3 * 2 * seq * hidden * ffn, bytes_accessed=3 * 2 * experts * hidden * ffn + 6 * seq * hidden, transcendentals=2 * seq * ffn),
    )(tile_start, pair_token, pair_gate, normed, w_gate, w_up, w_down)


def route(ids_full, gates_full, num_experts):
    seq = ids_full.shape[0]
    flat_ids = ids_full.reshape(2 * seq)
    sizes = jnp.sum((flat_ids[None, :] == jnp.arange(num_experts, dtype=jnp.int32)[:, None]).astype(jnp.int32), axis=1)
    tiles = (sizes + TILE - 1) // TILE
    tile_start = jnp.concatenate([jnp.zeros((1,), jnp.int32), jnp.cumsum(tiles).astype(jnp.int32)])
    spare = tiles * TILE - sizes
    filler = jnp.arange(TILE, dtype=jnp.int32)[None, :] < spare[:, None]
    filler_key = jnp.where(filler, jnp.arange(num_experts, dtype=jnp.int32)[:, None], num_experts).reshape(num_experts * TILE)
    keys = jnp.concatenate([flat_ids, filler_key])
    tokens = jnp.concatenate([jnp.arange(2 * seq, dtype=jnp.int32) // 2, jnp.full((num_experts * TILE,), seq, jnp.int32)])
    gates = jnp.concatenate([gates_full.reshape(2 * seq), jnp.zeros((num_experts * TILE,), jnp.float32)])
    _, pair_token, pair_gate = lax.sort((keys, tokens, gates), num_keys=1, is_stable=True)
    return tile_start, pair_token, pair_gate


def solution(mesh):
    token_spec = P(('rep', 'tok', 'mp'))
    row_spec = P(('rep', 'tok', 'mp'), None)
    head_weight = P(None, 'tok', 'mp', None)
    in_specs = (row_spec, token_spec, row_spec, row_spec, head_weight, head_weight, head_weight, P(None, 'mp', None, 'tok'), P(None, None, 'tok', 'mp'), P(None, None, 'tok', 'mp'), P(None, None, 'mp', 'tok'), P(None, None), P(None, None))

    def device_step(hidden_in, seg_ids, expert_ids, expert_gates, w_query, w_key, w_value, w_out, w_gate, w_up, w_down, gain_attn, gain_mlp):
        num_layers, depth, heads, head_dim = w_query.shape
        num_experts = w_gate.shape[1]
        hidden = hidden_in.shape[1]
        own_rows = hidden_in.shape[0]
        swap = [(0, 1), (1, 0)]
        my_mp = lax.axis_index('mp')

        seg_full = lax.all_gather(seg_ids, 'mp', axis=0, tiled=True)
        ids_full = lax.all_gather(expert_ids, 'mp', axis=0, tiled=True)
        gates_full = lax.all_gather(expert_gates, 'mp', axis=0, tiled=True)
        seq_len = seg_full.shape[0]
        starts = request_starts(seg_full)
        positions = jnp.arange(seq_len, dtype=jnp.int32) - starts
        cosines, sines = rope_tables(positions, head_dim)
        blocked = starts.reshape(seq_len // BLOCK, BLOCK)
        lo = blocked[:, 0] // BLOCK
        mid = jnp.minimum((blocked[:, -1] + BLOCK - 1) // BLOCK, jnp.arange(seq_len // BLOCK, dtype=jnp.int32))
        mid = jnp.maximum(mid, lo)
        tile_start, pair_token, pair_gate = route(ids_full, gates_full, num_experts)

        def combine(residual, part):
            own = lax.dynamic_slice(part, (my_mp * own_rows, 0), (own_rows, hidden))
            away = lax.dynamic_slice(part, ((1 - my_mp) * own_rows, 0), (own_rows, hidden)).astype(jnp.bfloat16)
            return residual + (own + lax.ppermute(away, 'mp', swap).astype(jnp.float32))

        residual = hidden_in.astype(jnp.float32)
        for layer in range(num_layers):
            packed = jnp.concatenate([
                w_query[layer].reshape(depth, heads * head_dim),
                w_key[layer].reshape(depth, heads * head_dim),
                w_value[layer].reshape(depth, heads * head_dim),
                w_out[layer].reshape(heads * head_dim, depth).T,
            ], axis=1)
            attn_weight = lax.all_gather(packed, 'tok', axis=0, tiled=True)
            gate_weight = lax.all_gather(w_gate[layer], 'tok', axis=0)
            up_weight = lax.all_gather(w_up[layer], 'tok', axis=0)
            down_weight = lax.all_gather(jnp.swapaxes(w_down[layer], 1, 2), 'tok', axis=0)
            normed = lax.all_gather(rms_norm(residual, gain_attn[layer]), 'mp', axis=0, tiled=True)
            attn_part = attention(normed, attn_weight, cosines, sines, positions[:, None], lo, mid, heads, head_dim)
            residual = combine(residual, attn_part)
            normed = lax.all_gather(rms_norm(residual, gain_mlp[layer]), 'mp', axis=0, tiled=True)
            mix_part = expert_mix(normed, tile_start, pair_token, pair_gate, gate_weight, up_weight, down_weight)
            residual = combine(residual, mix_part)
        return residual

    return jax.shard_map(device_step, mesh=mesh, in_specs=in_specs, out_specs=row_spec, check_vma=False)
```

time: 3060 us -> 1770 us (0.58)
  matrix products: 739 us -> 0 us
  other arithmetic: 735 us -> 65.5 us
  waiting for transfers between devices: 806 us -> 1040 us
  Pallas kernels: 313 us -> 539 us
  local copies, waits for them, and re-layouts: 269 us -> 68.4 us
  blocking collectives: 159 us -> 15.2 us
    dot_general x34 -> x0, matrix products: 719 us -> none  [the longest x16 350 us: one_block(): jnp.einsum('bhgd,shd->hgbs', q_block, k_rot, preferred_element_type=jnp.f...]
    reduce_scatter x4 -> x0, waiting for transfers between devices: 550 us -> none  [the longest x2 284 us: device_step(): lax.psum_scatter(mix_part, 'mp', scatter_dimension=0, tiled=True)]
    pallas_call x0 -> x4, Pallas kernels: none -> 539 us  [the longest x2 318 us: expert_mix(): pl.pallas_call(functools.partial(moe_kernel, seq=seq, hidden=hidden), nam...]
    reduce_sum x16 -> x1, other arithmetic: 362 us -> 0.18 us  [route(): jnp.sum((flat_ids[None, :] == jnp.arange(num_experts, dtype=jnp.int32)[:,...]
    all_gather x6 -> x8, waiting for transfers between devices: 201 us -> 527 us  [the longest x2 239 us: device_step(): lax.all_gather(jnp.swapaxes(w_down[layer], 1, 2), 'tok', axis=0)]
    another operation x6 -> x0, Pallas kernels: 312 us -> none
    ppermute x0 -> x4, waiting for transfers between devices: none -> 254 us  [combine(): return residual + (own + lax.ppermute(away, 'mp', swap).astype(jnp.float32))]
    scatter-add x3 -> x0, other arithmetic: 184 us -> none  [the longest x2 127 us: expert_mix(): jax.ops.segment_sum(down_out * pair_gate[:, None], pair_token, num_segmen...]
  transfers between devices with their start and end apart: 14 -> 16, of which waited for: 9 -> 14; matrix products, arithmetic and copies ran while one was open for 10% -> 5% of each run, Pallas kernels for 4% -> 6%
where the time goes in v1:
time: 1770 us; the launch traced here: 1760 us
  waiting for transfers between devices  1040 us (59%)
  Pallas kernels  539 us (30%)
  local copies, waits for them, and re-layouts  68.4 us (4%)
  other arithmetic  65.5 us (4%)
    pallas_call x2, Pallas kernels, expert_mix(): pl.pallas_call(functools.partial(moe_kernel, seq=seq, hidden=hidden), nam...  318 us
    ppermute x4, waiting for transfers between devices, combine(): return residual + (own + lax.ppermute(away, 'mp', swap).astype(jnp.float32))  254 us
    all_gather x2, waiting for transfers between devices, device_step(): lax.all_gather(jnp.swapaxes(w_down[layer], 1, 2), 'tok', axis=0)  239 us
    pallas_call x2, Pallas kernels, attention(): pl.pallas_call(functools.partial(attention_kernel, pairs=pairs, head_dim=...  221 us
    all_gather x2, waiting for transfers between devices, device_step(): up_weight = lax.all_gather(w_up[layer], 'tok', axis=0)  166 us
    all_gather x2, waiting for transfers between devices, device_step(): lax.all_gather(rms_norm(residual, gain_attn[layer]), 'mp', axis=0, tiled=...  156 us
    all_gather x2, waiting for transfers between devices, device_step(): gate_weight = lax.all_gather(w_gate[layer], 'tok', axis=0)  120 us
    all_gather x2, waiting for transfers between devices, device_step(): lax.all_gather(rms_norm(residual, gain_mlp[layer]), 'mp', axis=0, tiled=T...  102 us
  transfers between devices with their start and end apart: 16, of which 14 were waited for; matrix products, arithmetic and copies ran while one was open for 5% of the time, Pallas kernels for 6%

profile of v1, /device:TPU:0, one launch (start us, length us, event | category | flops | bytes accessed | tf_op | source)
XLA Modules:
  0.0 1760.1 jit_solution(17221677909021200586)
XLA Ops:
  24.3 5.7 all_gather.51
  33.2 9.3 fusion.3
  44.9 79.8 %all-gather.15.cloned.1.call-done.h_ref = bf16[4096,768]{1,0:T(8,128)(2,1)} async-done(((bf16[2048,768]{1,0:T(8,128)(2,1)}), bf16[4096,768]{1,0:T(8,128)(2,1)}) %all-gather.15.cloned.1.call-update) | async-done | bytes 6291472 | tf_op jit(solution)/shard_map/all_gather | solution.py:340
  126.2 110.6 %attn.2 = f32[4096,768]{1,0:T(8,128)} custom-call(s32[16]{0:T(128)S(1)} %get-tuple-element.25.lo_ref, s32[16]{0:T(128)S(1)} %get-tuple-element.24.mid_ref, bf16[4096,768]{1,0:T(8,128)(2,1)} %all-gather.15.cloned.1.call-done.h_ref, f32[4096,128]{1,0:T(8,128)S(1)} %copy-done.2, f32[4096,128]{1,0:T(8,128)S(1)} %get-tuple-element.40.sin_ref, ...), custom_call_target="tpu_custom_call" | custom-call | flops 16106127360 | bytes 18874368 | tf_op jit(solution)/shard_map/attn/pallas_call | solution.py:129
  236.8 4.8 dynamic-slice_convert_fusion.3
  242.7 63.9 %collective-permute-done = bf16[2048,768]{1,0:T(8,128)(2,1)S(1)} collective-permute-done((bf16[2048,768]{1,0:T(8,128)(2,1)}, bf16[2048,768]{1,0:T(8,128)(2,1)S(1)}, u32[]{:S(2)}, u32[]{:S(2)}) %collective-permute-start) | collective-permute-done | bytes 3145760 | tf_op jit(solution)/shard_map/ppermute | solution.py:326
  306.6 5.1 multiply_reduce_fusion.2
  316.7 13.3 all-gather.21.cloned.1.call-start
  330.0 8.2 fusion.14
  338.3 8.3 fusion.13
  346.6 8.3 slice_bitcast_fusion
  355.0 4.8 all_gather.54
  361.9 4.8 all_gather.55
  368.8 8.6 sort.31
  378.0 22.4 %all-gather.19.cloned.1.call-done.h_hbm = bf16[4096,768]{1,0:T(8,128)(2,1)} async-done(((bf16[2048,768]{1,0:T(8,128)(2,1)}), bf16[4096,768]{1,0:T(8,128)(2,1)}) %all-gather.19.cloned.1.call-update) | async-done | bytes 6291472 | tf_op jit(solution)/shard_map/all_gather | solution.py:343
  400.4 119.5 %all-gather.21.cloned.1.call-done.wg_ref = bf16[4,8,192,1536]{3,2,1,0:T(8,128)(2,1)} async-done(((bf16[1,8,192,1536]{3,2,1,0:T(8,128)(2,1)}), bf16[4,8,192,1536]{3,2,1,0:T(8,128)(2,1)}) %all-gather.21.cloned.1.call-update) | async-done | bytes 18874384 | tf_op jit(solution)/shard_map/all_gather | solution.py:337
  519.9 119.5 %all-gather.23.cloned.1.call-done.wu_ref = bf16[4,8,192,1536]{3,2,1,0:T(8,128)(2,1)} async-done(((bf16[1,8,192,1536]{3,2,1,0:T(8,128)(2,1)}), bf16[4,8,192,1536]{3,2,1,0:T(8,128)(2,1)}) %all-gather.23.cloned.1.call-update) | async-done | bytes 18874384 | tf_op jit(solution)/shard_map/all_gather | solution.py:338
  639.3 119.5 %all-gather.35.cloned.1.call-done = bf16[32,192,1536]{2,1,0:T(8,128)(2,1)} async-done(((bf16[8,192,1536]{2,1,0:T(8,128)(2,1)}), bf16[32,192,1536]{2,1,0:T(8,128)(2,1)}) %all-gather.35.cloned.1.call-update) | async-done | bytes 18874384 | tf_op jit(solution)/shard_map/all_gather | solution.py:339
  758.8 159.0 %moe.2 = f32[4096,768]{1,0:T(8,128)} custom-call(s32[9]{0:T(128)} %pad_add_fusion.1.tile_start_ref, s32[10240]{0:T(1024)} %get-tuple-element.10.tok_ref, f32[10240]{0:T(1024)} %get-tuple-element.11.gate_ref, bf16[4096,768]{1,0:T(8,128)(2,1)} %all-gather.19.cloned.1.call-done.h_hbm, bf16[4,8,192,1536]{3,2,1,0:T(8,128)(2,1)} %all-gather.21.cloned.1.call-done.wg_ref, ...), custom_call_target="tpu_custom_call" | custom-call | flops 57982058496 | bytes 75497472 | tf_op jit(solution)/shard_map/moe/pallas_call | solution.py:254
  928.1 59.6 %collective-permute-done.1 = bf16[2048,768]{1,0:T(8,128)(2,1)} collective-permute-done((bf16[2048,768]{1,0:T(8,128)(2,1)S(1)}, bf16[2048,768]{1,0:T(8,128)(2,1)}, u32[]{:S(2)}, u32[]{:S(2)}) %collective-permute-start.1) | collective-permute-done | bytes 3145760 | tf_op jit(solution)/shard_map/ppermute | solution.py:326
  987.7 6.7 multiply_reduce_fusion.1
  1001.5 76.2 %all-gather.25.cloned.1.call-done.h_ref = bf16[4096,768]{1,0:T(8,128)(2,1)} async-done(((bf16[2048,768]{1,0:T(8,128)(2,1)}), bf16[4096,768]{1,0:T(8,128)(2,1)}) %all-gather.25.cloned.1.call-update) | async-done | bytes 6291472 | tf_op jit(solution)/shard_map/all_gather | solution.py:340
  1079.3 110.8 %attn.3 = f32[4096,768]{1,0:T(8,128)} custom-call(s32[16]{0:T(128)S(1)} %get-tuple-element.25.lo_ref, s32[16]{0:T(128)S(1)} %get-tuple-element.24.mid_ref, bf16[4096,768]{1,0:T(8,128)(2,1)} %all-gather.25.cloned.1.call-done.h_ref, f32[4096,128]{1,0:T(8,128)S(1)} %copy-done.3, f32[4096,128]{1,0:T(8,128)S(1)} %copy-done.1, ...), custom_call_target="tpu_custom_call" | custom-call | flops 16106127360 | bytes 18874368 | tf_op jit(solution)/shard_map/attn/pallas_call | solution.py:129
  1193.7 64.7 %collective-permute-done.2 = bf16[2048,768]{1,0:T(8,128)(2,1)S(1)} collective-permute-done((bf16[2048,768]{1,0:T(8,128)(2,1)S(1)}, bf16[2048,768]{1,0:T(8,128)(2,1)S(1)}, u32[]{:S(2)}, u32[]{:S(2)}) %collective-permute-start.2) | collective-permute-done | bytes 3145760 | tf_op jit(solution)/shard_map/ppermute | solution.py:326
  1258.4 6.6 multiply_reduce_fusion
  1265.0 5.1 multiply_convert_fusion
  1270.1 46.6 %all-gather.33.cloned.1.call-done.wu_ref = bf16[4,8,192,1536]{3,2,1,0:T(8,128)(2,1)} async-done(((bf16[1,8,192,1536]{3,2,1,0:T(8,128)(2,1)}), bf16[4,8,192,1536]{3,2,1,0:T(8,128)(2,1)}) %all-gather.33.cloned.1.call-update) | async-done | bytes 18874384 | tf_op jit(solution)/shard_map/all_gather | solution.py:338
  1316.8 119.6 %all-gather.37.cloned.1.call-done = bf16[32,192,1536]{2,1,0:T(8,128)(2,1)} async-done(((bf16[8,192,1536]{2,1,0:T(8,128)(2,1)}), bf16[32,192,1536]{2,1,0:T(8,128)(2,1)}) %all-gather.37.cloned.1.call-update) | async-done | bytes 18874384 | tf_op jit(solution)/shard_map/all_gather | solution.py:339
  1436.4 79.6 %all-gather.29.cloned.1.call-done.h_hbm = bf16[4096,768]{1,0:T(8,128)(2,1)} async-done(((bf16[2048,768]{1,0:T(8,128)(2,1)}), bf16[4096,768]{1,0:T(8,128)(2,1)}) %all-gather.29.cloned.1.call-update) | async-done | bytes 6291472 | tf_op jit(solution)/shard_map/all_gather | solution.py:343
  1516.0 159.0 %moe.3 = f32[4096,768]{1,0:T(8,128)} custom-call(s32[9]{0:T(128)} %pad_add_fusion.1.tile_start_ref, s32[10240]{0:T(1024)} %get-tuple-element.10.tok_ref, f32[10240]{0:T(1024)} %get-tuple-element.11.gate_ref, bf16[4096,768]{1,0:T(8,128)(2,1)} %all-gather.29.cloned.1.call-done.h_hbm, bf16[4,8,192,1536]{3,2,1,0:T(8,128)(2,1)} %all-gather.31.cloned.1.call-done.wg_ref, ...), custom_call_target="tpu_custom_call" | custom-call | flops 57982058496 | bytes 75497472 | tf_op jit(solution)/shard_map/moe/pallas_call | solution.py:254
  1678.6 65.7 %collective-permute-done.3 = bf16[2048,768]{1,0:T(8,128)(2,1)S(1)} collective-permute-done((bf16[2048,768]{1,0:T(8,128)(2,1)S(1)}, bf16[2048,768]{1,0:T(8,128)(2,1)S(1)}, u32[]{:S(2)}, u32[]{:S(2)}) %collective-permute-start.3) | collective-permute-done | bytes 3145760 | tf_op jit(solution)/shard_map/ppermute | solution.py:326
  1744.2 8.6 add_add_fusion
  (111 shorter events, 62.0 us)
Async XLA Ops:
  6.5 14.5 copy-start.10
  6.5 14.5 copy-start.7
  6.5 38.3 %all-gather.17.cloned.1.call-start = ((), (), s32[]{:S(2)}) async-start(), calls=%async_computation.1 | async-start | bytes 2949120 | tf_op jit(solution)/shard_map/all_gather | solution.py:336
  21.0 103.7 %all-gather.15.cloned.1.call-start = ((), (), s32[]{:S(2)}) async-start(), calls=%async_computation | async-start | bytes 9437184 | tf_op jit(solution)/shard_map/all_gather | solution.py:340
  24.2 376.2 %all-gather.19.cloned.1.call-start = ((), (), s32[]{:S(2)}) async-start(), calls=%async_computation.2 | async-start | bytes 9437184 | tf_op jit(solution)/shard_map/all_gather | solution.py:343
  42.5 194.3 %copy-start = (f32[4096,128]{1,0:T(8,128)}, f32[4096,128]{1,0:T(8,128)S(1)}, u32[]{:S(2)}) copy-start(f32[4096,128]{1,0:T(8,128)S(1)} %get-tuple-element.40.sin_ref) | copy-start | bytes 6291460
  124.6 1.6 copy-start.2
  241.6 65.0 %collective-permute-start = (bf16[2048,768]{1,0:T(8,128)(2,1)}, bf16[2048,768]{1,0:T(8,128)(2,1)S(1)}, u32[]{:S(2)}, u32[]{:S(2)}) collective-permute-start(bf16[2048,768]{1,0:T(8,128)(2,1)} %dynamic-slice_convert_fusion.3), channel_id=1, source_target_pairs={{0,4},{4,0},{1,5},{5,1},{2,6},{6,2},{3,7},{7,3}} | collective-permute-start | bytes 9437192 | tf_op jit(solution)/shard_map/ppermute | solution.py:326
  311.7 2.7 copy-start.4
  316.7 203.1 %all-gather.21.cloned.1.call-start = ((), (), s32[]{:S(2)}) async-start(), calls=%async_computation.3 | async-start | bytes 23592960 | tf_op jit(solution)/shard_map/all_gather | solution.py:337
  338.2 301.1 %all-gather.23.cloned.1.call-start = ((), (), s32[]{:S(2)}) async-start(), calls=%async_computation.4 | async-start | bytes 23592960 | tf_op jit(solution)/shard_map/all_gather | solution.py:338
  346.6 8.4 copy-start.8
  346.6 412.2 %all-gather.35.cloned.1.call-start = ((), (), s32[]{:S(2)}) async-start(), calls=%async_computation.10 | async-start | bytes 23592960 | tf_op jit(solution)/shard_map/all_gather | solution.py:339
  354.9 7.0 copy-start.9
  354.9 646.5 %all-gather.27.cloned.1.call-start = ((), (), s32[]{:S(2)}) async-start(), calls=%async_computation.6 | async-start | bytes 2949120 | tf_op jit(solution)/shard_map/all_gather | solution.py:336
  920.9 66.7 %collective-permute-start.1 = (bf16[2048,768]{1,0:T(8,128)(2,1)S(1)}, bf16[2048,768]{1,0:T(8,128)(2,1)}, u32[]{:S(2)}, u32[]{:S(2)}) collective-permute-start(bf16[2048,768]{1,0:T(8,128)(2,1)S(1)} %dynamic-slice_convert_fusion.2), channel_id=1, source_target_pairs={{0,4},{4,0},{1,5},{5,1},{2,6},{6,2},{3,7},{7,3}} | collective-permute-start | bytes 9437192 | tf_op jit(solution)/shard_map/ppermute | solution.py:326
  928.0 149.6 %all-gather.25.cloned.1.call-start = ((), (), s32[]{:S(2)}) async-start(), calls=%async_computation.5 | async-start | bytes 9437184 | tf_op jit(solution)/shard_map/all_gather | solution.py:340
  994.3 2.7 copy-start.5
  999.3 270.8 %all-gather.31.cloned.1.call-start = ((), (), s32[]{:S(2)}) async-start(), calls=%async_computation.8 | async-start | bytes 23592960 | tf_op jit(solution)/shard_map/all_gather | solution.py:337
  999.4 78.3 %copy-start.1 = (f32[4096,128]{1,0:T(8,128)S(1)}, f32[4096,128]{1,0:T(8,128)}, u32[]{:S(2)}) copy-start(f32[4096,128]{1,0:T(8,128)} %copy-done) | copy-start | bytes 6291460
  1000.1 316.7 %all-gather.33.cloned.1.call-start = ((), (), s32[]{:S(2)}) async-start(), calls=%async_computation.9 | async-start | bytes 23592960 | tf_op jit(solution)/shard_map/all_gather | solution.py:338
  1000.7 435.8 %all-gather.37.cloned.1.call-start = ((), (), s32[]{:S(2)}) async-start(), calls=%async_computation.11 | async-start | bytes 23592960 | tf_op jit(solution)/shard_map/all_gather | solution.py:339
  1001.4 514.7 %all-gather.29.cloned.1.call-start = ((), (), s32[]{:S(2)}) async-start(), calls=%async_computation.7 | async-start | bytes 9437184 | tf_op jit(solution)/shard_map/all_gather | solution.py:343
  1077.7 1.6 copy-start.3
  1190.1 68.3 %copy-start.6 = (f32[2048,768]{1,0:T(8,128)S(1)}, f32[2048,768]{1,0:T(8,128)}, u32[]{:S(2)}) copy-start(f32[2048,768]{1,0:T(8,128)} %copy-done.5) | copy-start | bytes 18874372
  1193.3 65.1 %collective-permute-start.2 = (bf16[2048,768]{1,0:T(8,128)(2,1)S(1)}, bf16[2048,768]{1,0:T(8,128)(2,1)S(1)}, u32[]{:S(2)}, u32[]{:S(2)}) collective-permute-start(bf16[2048,768]{1,0:T(8,128)(2,1)S(1)} %dynamic-slice_convert_fusion.1), channel_id=1, source_target_pairs={{0,4},{4,0},{1,5},{5,1},{2,6},{6,2},{3,7},{7,3}} | collective-permute-start | bytes 9437192 | tf_op jit(solution)/shard_map/ppermute | solution.py:326
  1678.2 66.0 %collective-permute-start.3 = (bf16[2048,768]{1,0:T(8,128)(2,1)S(1)}, bf16[2048,768]{1,0:T(8,128)(2,1)S(1)}, u32[]{:S(2)}, u32[]{:S(2)}) collective-permute-start(bf16[2048,768]{1,0:T(8,128)(2,1)S(1)} %dynamic-slice_convert_fusion), channel_id=1, source_target_pairs={{0,4},{4,0},{1,5},{5,1},{2,6},{6,2},{3,7},{7,3}} | collective-permute-start | bytes 9437192 | tf_op jit(solution)/shard_map/ppermute | solution.py:326
Sparse Core Ops, SparseCore 0:
  21.1 23.7 all-gather.16
  46.4 78.2 all-gather.14
  316.8 83.4 all-gather.18
  401.8 118.0 all-gather.20
  521.2 118.0 all-gather.22
  640.7 118.0 all-gather.34
  928.2 19.9 all-gather.26
  999.5 78.1 all-gather.24
  1079.2 118.0 all-gather.30
  1198.7 118.0 all-gather.32
  1318.3 118.0 all-gather.36
  1437.8 78.2 all-gather.28

commit v2 on v1

v2 whole, which is shorter than its diff:
```python
import functools

import jax
import jax.numpy as jnp
from jax import lax
from jax.experimental import pallas as pl
from jax.experimental.pallas import tpu as pltpu
from jax.sharding import PartitionSpec as P


EPS = 1e-5
ROPE_BASE = 10000.0
BLOCK = 256
TILE = 256
BATCH = 16
MASKED = -1e30


def rms_norm(residual, gain):
    inv_rms = lax.rsqrt(jnp.mean(residual * residual, axis=-1, keepdims=True) + EPS)
    return (residual * inv_rms * gain.astype(jnp.float32)).astype(jnp.bfloat16)


def request_starts(seg_rows):
    token_index = jnp.arange(seg_rows.shape[0], dtype=jnp.int32)
    is_start = jnp.concatenate([jnp.ones((1,), dtype=jnp.bool_), seg_rows[1:] != seg_rows[:-1]])
    return lax.cummax(jnp.where(is_start, token_index, 0), axis=0)


def rope_tables(positions, head_dim):
    half = head_dim // 2
    lane = jnp.arange(2 * head_dim, dtype=jnp.int32)
    inv_freq = jnp.power(ROPE_BASE, -(lane % half).astype(jnp.float32) * 2.0 / head_dim)
    angles = positions.astype(jnp.float32)[:, None] * inv_freq[None, :]
    sign = jnp.where(lane % head_dim < half, -1.0, 1.0).astype(jnp.float32)
    return jnp.cos(angles), jnp.sin(angles) * sign


def attention_kernel(place_ref, lo_ref, mid_ref, own_ref, other_ref, cos_ref, sin_ref, pos_ref, w0, w1, w2, w3,
                     keep_ref, send_ref, w_scr, k_scr, v_scr, q_scr, m_scr, l_scr, acc_scr, w_sem, *, pairs, head_dim):
    i = pl.program_id(0)
    mine = place_ref[1] == i // (pl.num_programs(0) // 2)
    width = 2 * head_dim
    span = pairs * width
    half = head_dim // 2
    hidden = w_scr.shape[0] * w_scr.shape[1]

    @pl.when(i == 0)
    def _():
        copies = [pltpu.make_async_copy(piece, w_scr.at[place_ref[2 + q]], w_sem) for q, piece in enumerate((w0, w1, w2, w3))]
        for copy in copies:
            copy.start()
        for copy in copies:
            copy.wait()

    lane = lax.broadcasted_iota(jnp.int32, (BLOCK, width), 1)
    low_half = lane % head_dim < half
    first_head = lane < head_dim
    cosines = cos_ref[...]
    sines = sin_ref[...]
    h_block = jnp.where(mine, own_ref[...], other_ref[...])
    row0 = pl.multiple_of(i * BLOCK, BLOCK)

    def weight(col):
        return w_scr[:, :, pl.ds(col, width)].reshape(hidden, width)

    for p in range(pairs):
        q = jnp.dot(h_block, weight(p * width), preferred_element_type=jnp.float32)
        k = jnp.dot(h_block, weight(span + p * width), preferred_element_type=jnp.float32)
        v = jnp.dot(h_block, weight(2 * span + p * width), preferred_element_type=jnp.float32)
        q_turn = jnp.where(low_half, pltpu.roll(q, width - half, 1), pltpu.roll(q, half, 1))
        k_turn = jnp.where(low_half, pltpu.roll(k, width - half, 1), pltpu.roll(k, half, 1))
        q_rot = (q * cosines + q_turn * sines).astype(jnp.bfloat16).astype(jnp.float32) * (head_dim ** -0.5)
        k_rot = (k * cosines + k_turn * sines).astype(jnp.bfloat16)
        q_scr[2 * p] = jnp.where(first_head, q_rot, 0.0).astype(jnp.bfloat16)
        q_scr[2 * p + 1] = jnp.where(first_head, 0.0, q_rot).astype(jnp.bfloat16)
        k_scr[p, pl.ds(row0, BLOCK), :] = k_rot
        v_scr[p, pl.ds(2 * row0, BLOCK), :] = jnp.where(first_head, v, 0.0).astype(jnp.bfloat16)
        v_scr[p, pl.ds(2 * row0 + BLOCK, BLOCK), :] = jnp.where(first_head, 0.0, v).astype(jnp.bfloat16)

    m_scr[...] = jnp.full_like(m_scr, MASKED)
    l_scr[...] = jnp.zeros_like(l_scr)
    acc_scr[...] = jnp.zeros_like(acc_scr)

    def step(j, masked):
        col0 = pl.multiple_of(j * BLOCK, BLOCK)
        if masked:
            gap = (lax.broadcasted_iota(jnp.int32, (BLOCK, BLOCK), 0) - lax.broadcasted_iota(jnp.int32, (BLOCK, BLOCK), 1)) + (row0 - col0)
            allowed = (gap >= 0) & (gap <= pos_ref[...])
        for p in range(pairs):
            k_block = k_scr[p, pl.ds(col0, BLOCK), :]
            probs = []
            scales = []
            for e in range(2):
                hd = 2 * p + e
                s = lax.dot_general(q_scr[hd], k_block, (((1,), (1,)), ((), ())), preferred_element_type=jnp.float32)
                if masked:
                    s = jnp.where(allowed, s, MASKED)
                m_old = m_scr[hd]
                m_new = jnp.maximum(m_old, jnp.max(s, axis=1, keepdims=True))
                alpha = jnp.exp(m_old - m_new)
                m_wide = jnp.concatenate([m_new] * (BLOCK // width), axis=1)
                e_s = jnp.exp(s - m_wide)
                if masked:
                    e_s = jnp.where(allowed, e_s, 0.0)
                part = e_s[:, :width]
                for c in range(1, BLOCK // width):
                    part = part + e_s[:, c * width:(c + 1) * width]
                l_scr[hd] = l_scr[hd] * alpha + part
                m_scr[hd] = m_new
                probs.append(e_s.astype(jnp.bfloat16))
                scales.append(alpha)
            pv = jnp.dot(jnp.concatenate(probs, axis=1), v_scr[p, pl.ds(2 * col0, 2 * BLOCK), :], preferred_element_type=jnp.float32)
            acc_scr[p] = acc_scr[p] * jnp.where(first_head, scales[0], scales[1]) + pv

    def masked_step(j, carry):
        step(j, True)
        return carry

    def plain_step(j, carry):
        step(j, False)
        return carry

    lax.fori_loop(lo_ref[i], mid_ref[i], masked_step, 0)
    lax.fori_loop(mid_ref[i], i, plain_step, 0)
    step(i, True)

    outs = []
    for p in range(pairs):
        l0 = jnp.sum(l_scr[2 * p], axis=1, keepdims=True)
        l1 = jnp.sum(l_scr[2 * p + 1], axis=1, keepdims=True)
        outs.append((acc_scr[p] / jnp.where(first_head, l0, l1)).astype(jnp.bfloat16))
    o = jnp.concatenate(outs, axis=1)
    w_o = w_scr[:, :, pl.ds(3 * span, span)].reshape(hidden, span)
    out = lax.dot_general(o, w_o, (((1,), (1,)), ((), ())), preferred_element_type=jnp.float32)

    @pl.when(mine)
    def _():
        keep_ref[...] = out

    @pl.when(jnp.logical_not(mine))
    def _():
        send_ref[...] = out.astype(jnp.bfloat16)


def attention(own, other, pieces, cosines, sines, positions, place, lo, mid, heads, head_dim):
    rows, hidden = own.shape
    seq = 2 * rows
    pairs = heads // 2
    width = 2 * head_dim
    blocks = seq // BLOCK
    span = pairs * width
    per = blocks // 2
    flops = 2 * seq * hidden * 4 * span + 4 * seq * (seq // 4) * span

    def own_index(i, place, *_):
        return (jnp.clip(i - per * place[1], 0, per - 1), 0)

    def other_index(i, place, *_):
        return (jnp.clip(i - per * (1 - place[1]), 0, per - 1), 0)

    anywhere = pl.BlockSpec(memory_space=pl.ANY)
    return pl.pallas_call(
        functools.partial(attention_kernel, pairs=pairs, head_dim=head_dim),
        name='attn',
        out_shape=(jax.ShapeDtypeStruct((rows, hidden), jnp.float32), jax.ShapeDtypeStruct((rows, hidden), jnp.bfloat16)),
        grid_spec=pltpu.PrefetchScalarGridSpec(
            num_scalar_prefetch=3,
            grid=(blocks,),
            in_specs=[
                pl.BlockSpec((BLOCK, hidden), own_index),
                pl.BlockSpec((BLOCK, hidden), other_index),
                pl.BlockSpec((BLOCK, width), lambda i, *_: (i, 0)),
                pl.BlockSpec((BLOCK, width), lambda i, *_: (i, 0)),
                pl.BlockSpec((BLOCK, 1), lambda i, *_: (i, 0)),
                anywhere, anywhere, anywhere, anywhere,
            ],
            out_specs=(pl.BlockSpec((BLOCK, hidden), own_index), pl.BlockSpec((BLOCK, hidden), other_index)),
            scratch_shapes=[
                pltpu.VMEM((len(pieces),) + pieces[0].shape, jnp.bfloat16),
                pltpu.VMEM((pairs, seq, width), jnp.bfloat16),
                pltpu.VMEM((pairs, 2 * seq, width), jnp.bfloat16),
                pltpu.VMEM((heads, BLOCK, width), jnp.bfloat16),
                pltpu.VMEM((heads, BLOCK, width), jnp.float32),
                pltpu.VMEM((heads, BLOCK, width), jnp.float32),
                pltpu.VMEM((pairs, BLOCK, width), jnp.float32),
                pltpu.SemaphoreType.DMA,
            ],
        ),
        compiler_params=pltpu.CompilerParams(dimension_semantics=('arbitrary',), vmem_limit_bytes=48 * 1024 * 1024),
        cost_estimate=pl.CostEstimate(flops=flops, bytes_accessed=6 * seq * hidden, transcendentals=seq * (seq // 4) * heads),
    )(place, lo, mid, own, other, cosines, sines, positions, *pieces)


def moe_kernel(place_ref, tile_start_ref, tok_ref, gate_ref, *refs, seq, hidden, base_expert, experts, first, last):
    own_hbm, other_hbm, w0, w1, w2, w3 = refs[:6]
    refs = refs[6:]
    if not first:
        acc_in, refs = refs[0], refs[1:]
    if last:
        keep_hbm, send_hbm = refs[:2]
        refs = refs[2:]
    else:
        acc_out, refs = refs[0], refs[1:]
    h_scr, acc_scr, x_scr, y_scr, a_scr, w_scr, in_scr, keep_scr, send_scr, in_sem, keep_sem, send_sem, w_sem, acc_sem = refs
    groups = hidden // 128
    chunks = seq // TILE
    half = chunks // 2
    ffn = w_scr.shape[-1]
    step_n = 512
    my_mp = place_ref[1]
    pieces = (w0, w1, w2, w3)

    def rows_of(c):
        return pl.ds(pl.multiple_of(c * TILE, TILE), TILE)

    def weights(e, slot):
        copies = []
        for q, piece in enumerate(pieces):
            for t in range(3):
                copies.append(pltpu.make_async_copy(piece.at[t * experts + e], w_scr.at[slot, t, place_ref[2 + q]], w_sem.at[slot]))
        return copies

    for copy in weights(0, 0):
        copy.start()
    if not first:
        acc_copy = pltpu.make_async_copy(acc_in, acc_scr.at[pl.ds(0, seq)], acc_sem)
        acc_copy.start()

    def fetch(c, slot, act):
        mine = my_mp == c // half
        local = lax.rem(c, half)

        @pl.when(mine)
        def _():
            act(pltpu.make_async_copy(own_hbm.at[rows_of(local), :], in_scr.at[slot], in_sem.at[slot]))

        @pl.when(jnp.logical_not(mine))
        def _():
            act(pltpu.make_async_copy(other_hbm.at[rows_of(local), :], in_scr.at[slot], in_sem.at[slot]))

    fetch(0, 0, lambda copy: copy.start())

    def load(c, carry):
        slot = lax.rem(c, 2)

        @pl.when(c + 1 < chunks)
        def _():
            fetch(c + 1, 1 - slot, lambda copy: copy.start())

        fetch(c, slot, lambda copy: copy.wait())
        rows = in_scr[slot].astype(jnp.float32)
        for g in range(groups):
            h_scr[rows_of(c), g, :] = rows[:, g * 128:(g + 1) * 128]
        if first:
            acc_scr[rows_of(c)] = jnp.zeros((TILE, 8, 128), jnp.float32)
        return carry

    lax.fori_loop(0, chunks, load, 0)
    h_scr[pl.ds(seq, 8)] = jnp.zeros((8, 8, 128), jnp.float32)
    acc_scr[pl.ds(seq, 8)] = jnp.zeros((8, 8, 128), jnp.float32)
    if not first:
        acc_copy.wait()

    def gather(t, slot, lo, hi):
        first_row = t * TILE
        for b in range(lo, hi, BATCH):
            vals = [h_scr[tok_ref[first_row + b + r]] for r in range(BATCH)]
            for r in range(BATCH):
                x_scr[slot, b + r] = vals[r]

    def scatter(t, slot, lo, hi):
        first_row = t * TILE
        for b in range(lo, hi, BATCH):
            toks = [tok_ref[first_row + b + r] for r in range(BATCH)]
            vals = [acc_scr[toks[r]] + gate_ref[first_row + b + r] * y_scr[slot, b + r] for r in range(BATCH)]
            for r in range(BATCH):
                acc_scr[toks[r]] = vals[r]

    begin = tile_start_ref[base_expert]
    end = tile_start_ref[base_expert + experts]
    y_scr[lax.rem(begin + 1, 2)] = jnp.zeros(y_scr.shape[1:], jnp.float32)

    def gather_loop(b, carry):
        vals = [h_scr[tok_ref[begin * TILE + b * BATCH + r]] for r in range(BATCH)]
        for r in range(BATCH):
            x_scr[lax.rem(begin, 2), b * BATCH + r] = vals[r]
        return carry

    lax.fori_loop(0, TILE // BATCH, gather_loop, 0)

    def expert_body(e, carry):
        slot_w = lax.rem(e, 2)

        @pl.when(e + 1 < experts)
        def _():
            for copy in weights(e + 1, 1 - slot_w):
                copy.start()

        for copy in weights(e, slot_w):
            copy.wait()

        def tile_body(t, carry):
            slot = lax.rem(t, 2)
            before = jnp.maximum(t - 1, 0)
            x = jnp.concatenate([x_scr[slot, :, g, :] for g in range(groups)], axis=1).astype(jnp.bfloat16)
            parts = ffn // step_n
            cut = [TILE * n // parts // BATCH * BATCH for n in range(parts)] + [TILE]
            for n in range(parts):
                cols = pl.ds(n * step_n, step_n)
                gate_pre = jnp.dot(x, w_scr[slot_w, 0, :, :, cols].reshape(hidden, step_n), preferred_element_type=jnp.float32)
                up_pre = jnp.dot(x, w_scr[slot_w, 1, :, :, cols].reshape(hidden, step_n), preferred_element_type=jnp.float32)
                a_scr[:, cols] = (gate_pre * jax.nn.sigmoid(gate_pre) * up_pre).astype(jnp.bfloat16)
                scatter(before, 1 - slot, cut[n], cut[n + 1])
                gather(t + 1, 1 - slot, cut[n], cut[n + 1])
            y = lax.dot_general(a_scr[...], w_scr[slot_w, 2].reshape(hidden, ffn), (((1,), (1,)), ((), ())), preferred_element_type=jnp.float32)
            for g in range(groups):
                y_scr[slot, :, g, :] = y[:, g * 128:(g + 1) * 128]
            return carry

        lax.fori_loop(tile_start_ref[base_expert + e], tile_start_ref[base_expert + e + 1], tile_body, 0)
        return carry

    lax.fori_loop(0, experts, expert_body, 0)

    @pl.when(end > begin)
    def _():
        final = end - 1

        def scatter_loop(b, carry):
            first_row = final * TILE + b * BATCH
            toks = [tok_ref[first_row + r] for r in range(BATCH)]
            vals = [acc_scr[toks[r]] + gate_ref[first_row + r] * y_scr[lax.rem(final, 2), b * BATCH + r] for r in range(BATCH)]
            for r in range(BATCH):
                acc_scr[toks[r]] = vals[r]
            return carry

        lax.fori_loop(0, TILE // BATCH, scatter_loop, 0)

    if not last:
        copy = pltpu.make_async_copy(acc_scr.at[pl.ds(0, seq)], acc_out, acc_sem)
        copy.start()
        copy.wait()
        return

    def flush(scr, hbm, sem, c, slot):
        return pltpu.make_async_copy(scr.at[slot], hbm.at[rows_of(c), :], sem.at[slot])

    for which, (scr, hbm, sem) in enumerate(((send_scr, send_hbm, send_sem), (keep_scr, keep_hbm, keep_sem))):
        offset = (my_mp if which else 1 - my_mp) * half

        def store(c, carry, scr=scr, hbm=hbm, sem=sem, offset=offset):
            slot = lax.rem(c, 2)

            @pl.when(c >= 2)
            def _():
                flush(scr, hbm, sem, c - 2, slot).wait()

            for g in range(groups):
                scr[slot, :, pl.ds(g * 128, 128)] = acc_scr[rows_of(offset + c), g, :].astype(scr.dtype)
            flush(scr, hbm, sem, c, slot).start()
            return carry

        lax.fori_loop(0, half, store, 0)
        for c in (half - 2, half - 1):
            flush(scr, hbm, sem, c, c % 2).wait()


def expert_mix(own, other, place, tile_start, pair_token, pair_gate, pieces, base_expert, acc, last):
    rows, hidden = own.shape
    seq = 2 * rows
    experts = pieces[0].shape[0] // 3
    depth, ffn = pieces[0].shape[1:]
    anywhere = pl.BlockSpec(memory_space=pl.ANY)
    first = acc is None
    operands = [own, other, *pieces] + ([] if first else [acc])
    if last:
        out_shape = (jax.ShapeDtypeStruct((rows, hidden), jnp.float32), jax.ShapeDtypeStruct((rows, hidden), jnp.bfloat16))
        out_specs = (anywhere, anywhere)
    else:
        out_shape = jax.ShapeDtypeStruct((seq, 8, 128), jnp.float32)
        out_specs = anywhere
    return pl.pallas_call(
        functools.partial(moe_kernel, seq=seq, hidden=hidden, base_expert=base_expert, experts=experts, first=first, last=last),
        name='moe',
        out_shape=out_shape,
        grid_spec=pltpu.PrefetchScalarGridSpec(
            num_scalar_prefetch=4,
            grid=(1,),
            in_specs=[anywhere] * len(operands),
            out_specs=out_specs,
            scratch_shapes=[
                pltpu.VMEM((seq + 8, 8, 128), jnp.float32),
                pltpu.VMEM((seq + 8, 8, 128), jnp.float32),
                pltpu.VMEM((2, TILE, 8, 128), jnp.float32),
                pltpu.VMEM((2, TILE, 8, 128), jnp.float32),
                pltpu.VMEM((TILE, ffn), jnp.bfloat16),
                pltpu.VMEM((2, 3, len(pieces), depth, ffn), jnp.bfloat16),
                pltpu.VMEM((2, TILE, hidden), jnp.bfloat16),
                pltpu.VMEM((2, TILE, hidden), jnp.float32),
                pltpu.VMEM((2, TILE, hidden), jnp.bfloat16),
                pltpu.SemaphoreType.DMA((2,)),
                pltpu.SemaphoreType.DMA((2,)),
                pltpu.SemaphoreType.DMA((2,)),
                pltpu.SemaphoreType.DMA((2,)),
                pltpu.SemaphoreType.DMA,
            ],
        ),
        compiler_params=pltpu.CompilerParams(dimension_semantics=('arbitrary',), vmem_limit_bytes=63 * 1024 * 1024),
        cost_estimate=pl.CostEstimate(flops=3 * 2 * seq * hidden * ffn, bytes_accessed=6 * experts * hidden * ffn + 20 * seq * hidden, transcendentals=seq * ffn),
    )(place, tile_start, pair_token, pair_gate, *operands)


def route(ids_full, gates_full, num_experts):
    seq = ids_full.shape[0]
    flat_ids = ids_full.reshape(2 * seq)
    sizes = jnp.sum((flat_ids[None, :] == jnp.arange(num_experts, dtype=jnp.int32)[:, None]).astype(jnp.int32), axis=1)
    tiles = (sizes + TILE - 1) // TILE
    tile_start = jnp.concatenate([jnp.zeros((1,), jnp.int32), jnp.cumsum(tiles).astype(jnp.int32)])
    spare = tiles * TILE - sizes
    filler = jnp.arange(TILE, dtype=jnp.int32)[None, :] < spare[:, None]
    filler_key = jnp.where(filler, jnp.arange(num_experts, dtype=jnp.int32)[:, None], num_experts).reshape(num_experts * TILE)
    keys = jnp.concatenate([flat_ids, filler_key])
    tokens = jnp.concatenate([jnp.arange(2 * seq, dtype=jnp.int32) // 2, jnp.full((num_experts * TILE,), seq, jnp.int32)])
    gates = jnp.concatenate([gates_full.reshape(2 * seq), jnp.zeros((num_experts * TILE,), jnp.float32)])
    _, pair_token, pair_gate = lax.sort((keys, tokens, gates), num_keys=1, is_stable=True)
    return tile_start, pair_token, pair_gate


def solution(mesh):
    token_spec = P(('rep', 'tok', 'mp'))
    row_spec = P(('rep', 'tok', 'mp'), None)
    head_weight = P(None, 'tok', 'mp', None)
    in_specs = (row_spec, token_spec, row_spec, row_spec, head_weight, head_weight, head_weight, P(None, 'mp', None, 'tok'), P(None, None, 'tok', 'mp'), P(None, None, 'tok', 'mp'), P(None, None, 'mp', 'tok'), P(None, None), P(None, None))

    def device_step(hidden_in, seg_ids, expert_ids, expert_gates, w_query, w_key, w_value, w_out, w_gate, w_up, w_down, gain_attn, gain_mlp):
        num_layers, depth, heads, head_dim = w_query.shape
        num_experts = w_gate.shape[1]
        halves = 2
        group = num_experts // halves
        swap = [(0, 1), (1, 0)]
        across = [(t, t ^ 2) for t in range(4)]
        beside = [(t, t ^ 1) for t in range(4)]
        my_mp = lax.axis_index('mp')
        my_tok = lax.axis_index('tok')
        place = jnp.stack([my_tok, my_mp] + [my_tok ^ q for q in range(4)]).astype(jnp.int32)

        def spread(own):
            far = lax.ppermute(own, 'tok', across)
            side = lax.ppermute(own, 'tok', beside)
            near = lax.ppermute(far, 'tok', beside)
            return own, side, far, near

        def exchange(rows):
            return lax.ppermute(rows, 'mp', swap)

        def pack_attn(layer):
            return jnp.concatenate([
                w_query[layer].reshape(depth, heads * head_dim),
                w_key[layer].reshape(depth, heads * head_dim),
                w_value[layer].reshape(depth, heads * head_dim),
                w_out[layer].reshape(heads * head_dim, depth).T,
            ], axis=1)

        def pack_experts(layer, part):
            which = slice(part * group, (part + 1) * group)
            return jnp.concatenate([w_gate[layer, which], w_up[layer, which], jnp.swapaxes(w_down[layer, which], 1, 2)], axis=0)

        residual = hidden_in.astype(jnp.float32)
        seg_full = lax.all_gather(seg_ids, 'mp', axis=0, tiled=True)
        ids_full = lax.all_gather(expert_ids, 'mp', axis=0, tiled=True)
        gates_full = lax.all_gather(expert_gates, 'mp', axis=0, tiled=True)
        seq_len = seg_full.shape[0]
        starts = request_starts(seg_full)
        positions = jnp.arange(seq_len, dtype=jnp.int32) - starts
        cosines, sines = rope_tables(positions, head_dim)
        blocked = starts.reshape(seq_len // BLOCK, BLOCK)
        lo = blocked[:, 0] // BLOCK
        mid = jnp.minimum((blocked[:, -1] + BLOCK - 1) // BLOCK, jnp.arange(seq_len // BLOCK, dtype=jnp.int32))
        mid = jnp.maximum(mid, lo)
        tile_start, pair_token, pair_gate = route(ids_full, gates_full, num_experts)

        attn_pieces = []
        expert_pieces = []
        for layer in range(num_layers):
            attn_pieces.append(spread(pack_attn(layer)))
            expert_pieces.append([spread(pack_experts(layer, part)) for part in range(halves)])

        for layer in range(num_layers):
            normed = rms_norm(residual, gain_attn[layer])
            other = exchange(normed)
            keep, send = attention(normed, other, attn_pieces[layer], cosines, sines, positions[:, None], place, lo, mid, heads, head_dim)
            residual = residual + (keep + exchange(send).astype(jnp.float32))
            normed = rms_norm(residual, gain_mlp[layer])
            other = exchange(normed)
            acc = None
            for part in range(halves):
                acc = expert_mix(normed, other, place, tile_start, pair_token, pair_gate, expert_pieces[layer][part], part * group, acc, part == halves - 1)
            keep, send = acc
            residual = residual + (keep + exchange(send).astype(jnp.float32))
        return residual


    return jax.shard_map(device_step, mesh=mesh, in_specs=in_specs, out_specs=row_spec, check_vma=False)
```

time: 1770 us -> 1430 us (0.81)
  the two profiles are of different devices: /device:TPU:0 before, /device:TPU:3 now
where the time goes in v2:
time: 1430 us
  Pallas kernels  607 us (42%)
  waiting for transfers between devices  538 us (38%)
  blocking collectives  137 us (10%)
  other arithmetic  78.2 us (5%)
  local copies, waits for them, and re-layouts  35.6 us (2%)
  starting transfers between devices  28 us (2%)
    pallas_call x4, Pallas kernels, expert_mix(): pl.pallas_call(functools.partial(moe_kernel, seq=seq, hidden=hidden, base...  359 us
    ppermute x6, waiting for transfers between devices, spread(): far = lax.ppermute(own, 'tok', across)  320 us
    pallas_call x2, Pallas kernels, attention(): pl.pallas_call(functools.partial(attention_kernel, pairs=pairs, head_dim=...  248 us
    ppermute x8, waiting for transfers between devices, exchange(): return lax.ppermute(rows, 'mp', swap)  216 us
    all_gather x1, blocking collectives, device_step(): ids_full = lax.all_gather(expert_ids, 'mp', axis=0, tiled=True)  68.9 us
    all_gather x1, blocking collectives, device_step(): seg_full = lax.all_gather(seg_ids, 'mp', axis=0, tiled=True)  65 us
  transfers between devices with their start and end apart: 26, of which 7 were waited for; matrix products, arithmetic and copies ran while one was open for 7% of the time, Pallas kernels for 29%

profile of v2, /device:TPU:3, one launch (start us, length us, event | category | flops | bytes accessed | tf_op | source)
XLA Modules:
  0.0 1425.2 jit_solution(18281662756485544597)
XLA Ops:
  7.6 5.7 slice_bitcast_fusion
  13.4 10.6 slice_bitcast_fusion.1
  24.0 3.5 pad_maximum_fusion.1.refs_2_
  33.6 3.4 pad_maximum_fusion.refs_2_
  37.2 65.0 %all_gather.9 = s32[4096]{0:T(1024)S(1)} all-gather(s32[2048]{0:T(1024)S(1)} %copy-done.23), channel_id=1, replica_groups=mesh['rep'=1,'mp'=2,'tok'=4] {'mp'}, dimensions={0}, use_global_device_ids=true | all-gather | bytes 24576 | tf_op jit(solution)/shard_map/all_gather | solution.py:470
  105.0 9.2 fusion.3
  115.3 3.1 iota_subtract_fusion.pos_ref
  121.8 124.5 %attn.2 = (f32[2048,768]{1,0:T(8,128)}, bf16[2048,768]{1,0:T(8,128)(2,1)}) custom-call(s32[6]{0:T(128)S(1)} %stack.24.place_ref, s32[16]{0:T(128)S(1)} %get-tuple-element.39.lo_ref, s32[16]{0:T(128)S(1)} %get-tuple-element.38.mid_ref, bf16[2048,768]{1,0:T(8,128)(2,1)} %fusion.2.own_ref, bf16[2048,768]{1,0:T(8,128)(2,1)} %collective-permute-done.other_ref, ...), custom_call_target="tpu_custom_call" | custom-call | flops 16106127360 | bytes 18874368 | tf_op jit(solution)/shard_map/attn/pallas_call | solution.py:163
  248.1 85.8 %collective-permute-done.7.refs_4_ = bf16[12,192,1536]{2,1,0:T(8,128)(2,1)} collective-permute-done((bf16[12,192,1536]{2,1,0:T(8,128)(2,1)}, bf16[12,192,1536]{2,1,0:T(8,128)(2,1)}, u32[]{:S(2)}, u32[]{:S(2)}) %collective-permute-start.7) | collective-permute-done | bytes 7077920 | tf_op jit(solution)/shard_map/ppermute | solution.py:449
  334.5 5.4 multiply_reduce_fusion.2
  340.3 2.6 multiply_convert_fusion.2.refs_0_
  344.3 68.9 %all_gather.10 = s32[4096,2]{0,1:T(2,128)S(1)} all-gather(s32[2048,2]{0,1:T(2,128)S(1)} %copy-done.19), channel_id=1, replica_groups=mesh['rep'=1,'mp'=2,'tok'=4] {'mp'}, dimensions={0}, use_global_device_ids=true | all-gather | bytes 49152 | tf_op jit(solution)/shard_map/all_gather | solution.py:471
  415.3 3.4 all_gather.11
  420.9 8.6 sort.31
  430.0 84.3 %moe.4.refs_6_ = f32[4096,8,128]{2,1,0:T(8,128)} custom-call(s32[6]{0:T(128)} %copy-done.2, s32[9]{0:T(128)} %pad_add_fusion.1.tile_start_ref, s32[10240]{0:T(1024)} %get-tuple-element.20.tok_ref, f32[10240]{0:T(1024)} %get-tuple-element.21.gate_ref, bf16[2048,768]{1,0:T(8,128)(2,1)} %multiply_convert_fusion.2.refs_0_, ...), custom_call_target="tpu_custom_call" | custom-call | flops 28991029248 | bytes 91226112 | tf_op jit(solution)/shard_map/moe/pallas_call | solution.py:383
  514.3 95.5 %moe.5 = (f32[2048,768]{1,0:T(8,128)}, bf16[2048,768]{1,0:T(8,128)(2,1)}) custom-call(s32[6]{0:T(128)} %copy-done.2, s32[9]{0:T(128)} %pad_add_fusion.1.tile_start_ref, s32[10240]{0:T(1024)} %get-tuple-element.20.tok_ref, f32[10240]{0:T(1024)} %get-tuple-element.21.gate_ref, bf16[2048,768]{1,0:T(8,128)(2,1)} %multiply_convert_fusion.2.refs_0_, ...), custom_call_target="tpu_custom_call" | custom-call | flops 28991029248 | bytes 91226112 | tf_op jit(solution)/shard_map/moe/pallas_call | solution.py:383
  612.0 7.3 pad_maximum_fusion.3.refs_2_
  619.3 56.1 %collective-permute-done.12 = bf16[2048,768]{1,0:T(8,128)(2,1)S(1)} collective-permute-done((bf16[2048,768]{1,0:T(8,128)(2,1)}, bf16[2048,768]{1,0:T(8,128)(2,1)S(1)}, u32[]{:S(2)}, u32[]{:S(2)}) %collective-permute-start.12) | collective-permute-done | bytes 3145760 | tf_op jit(solution)/shard_map/ppermute | solution.py:455
  675.5 3.9 multiply_reduce_fusion.1
  685.8 3.5 pad_maximum_fusion.2.refs_2_
  691.4 6.3 collective-permute-start.14
  697.8 234.4 %collective-permute-done.15.w2 = bf16[192,1536]{1,0:T(8,128)(2,1)S(1)} collective-permute-done((bf16[192,1536]{1,0:T(8,128)(2,1)S(1)}, bf16[192,1536]{1,0:T(8,128)(2,1)S(1)}, u32[]{:S(2)}, u32[]{:S(2)}) %collective-permute-start.15) | collective-permute-done | bytes 589856 | tf_op jit(solution)/shard_map/ppermute | solution.py:449
  932.2 6.4 collective-permute-start.16
  940.2 123.4 %attn.3 = (f32[2048,768]{1,0:T(8,128)}, bf16[2048,768]{1,0:T(8,128)(2,1)}) custom-call(s32[6]{0:T(128)S(1)} %copy-done.3, s32[16]{0:T(128)S(1)} %get-tuple-element.39.lo_ref, s32[16]{0:T(128)S(1)} %get-tuple-element.38.mid_ref, bf16[2048,768]{1,0:T(8,128)(2,1)} %multiply_convert_fusion.1.own_ref, bf16[2048,768]{1,0:T(8,128)(2,1)} %collective-permute-done.13.other_ref, ...), custom_call_target="tpu_custom_call" | custom-call | flops 16106127360 | bytes 18874368 | tf_op jit(solution)/shard_map/attn/pallas_call | solution.py:163
  1064.7 54.0 %collective-permute-done.17 = bf16[2048,768]{1,0:T(8,128)(2,1)S(1)} collective-permute-done((bf16[2048,768]{1,0:T(8,128)(2,1)}, bf16[2048,768]{1,0:T(8,128)(2,1)S(1)}, u32[]{:S(2)}, u32[]{:S(2)}) %collective-permute-start.17) | collective-permute-done | bytes 3145760 | tf_op jit(solution)/shard_map/ppermute | solution.py:455
  1118.8 6.7 multiply_reduce_fusion
  1125.4 3.4 multiply_convert_fusion.refs_0_
  1130.5 51.0 %collective-permute-done.18.refs_1_ = bf16[2048,768]{1,0:T(8,128)(2,1)} collective-permute-done((bf16[2048,768]{1,0:T(8,128)(2,1)S(1)}, bf16[2048,768]{1,0:T(8,128)(2,1)}, u32[]{:S(2)}, u32[]{:S(2)}) %collective-permute-start.18) | collective-permute-done | bytes 3145760 | tf_op jit(solution)/shard_map/ppermute | solution.py:455
  1181.5 84.4 %moe.6.refs_6_ = f32[4096,8,128]{2,1,0:T(8,128)} custom-call(s32[6]{0:T(128)} %copy-done.2, s32[9]{0:T(128)} %pad_add_fusion.1.tile_start_ref, s32[10240]{0:T(1024)} %get-tuple-element.20.tok_ref, f32[10240]{0:T(1024)} %get-tuple-element.21.gate_ref, bf16[2048,768]{1,0:T(8,128)(2,1)} %copy-done.15, bf16[2048,768]{1,0:T(8,128)(2,1)} %collective-permute-done.18.refs_1_, ...), custom_call_target="tpu_custom_call" | custom-call | flops 28991029248 | bytes 91226112 | tf_op jit(solution)/shard_map/moe/pallas_call | solution.py:383
  1265.9 95.1 %moe.7 = (f32[2048,768]{1,0:T(8,128)}, bf16[2048,768]{1,0:T(8,128)(2,1)}) custom-call(s32[6]{0:T(128)} %copy-done.2, s32[9]{0:T(128)} %pad_add_fusion.1.tile_start_ref, s32[10240]{0:T(1024)} %get-tuple-element.20.tok_ref, f32[10240]{0:T(1024)} %get-tuple-element.21.gate_ref, bf16[2048,768]{1,0:T(8,128)(2,1)} %copy-done.15, ...), custom_call_target="tpu_custom_call" | custom-call | flops 28991029248 | bytes 91226112 | tf_op jit(solution)/shard_map/moe/pallas_call | solution.py:383
  1361.7 55.0 %collective-permute-done.25 = bf16[2048,768]{1,0:T(8,128)(2,1)S(1)} collective-permute-done((bf16[2048,768]{1,0:T(8,128)(2,1)}, bf16[2048,768]{1,0:T(8,128)(2,1)S(1)}, u32[]{:S(2)}, u32[]{:S(2)}) %collective-permute-start.25) | collective-permute-done | bytes 3145760 | tf_op jit(solution)/shard_map/ppermute | solution.py:455
  1416.7 8.3 add_add_fusion
  (152 shorter events, 45.7 us)
Async XLA Ops:
  6.9 107.4 %collective-permute-start.2 = (bf16[192,1536]{1,0:T(8,128)(2,1)S(1)}, bf16[192,1536]{1,0:T(8,128)(2,1)S(1)}, u32[]{:S(2)}, u32[]{:S(2)}) collective-permute-start(bf16[192,1536]{1,0:T(8,128)(2,1)S(1)} %pad_maximum_fusion.4.w0), channel_id=1, source_target_pairs={{0,2},{1,3},{2,0},{3,1},{4,6},{5,7},{6,4},{7,5}} | collective-permute-start | bytes 1769480 | tf_op jit(solution)/shard_map/ppermute | solution.py:449
  6.9 114.8 %collective-permute-start.1 = (bf16[192,1536]{1,0:T(8,128)(2,1)S(1)}, bf16[192,1536]{1,0:T(8,128)(2,1)}, u32[]{:S(2)}, u32[]{:S(2)}) collective-permute-start(bf16[192,1536]{1,0:T(8,128)(2,1)S(1)} %pad_maximum_fusion.4.w0), channel_id=1, source_target_pairs={{0,1},{1,0},{2,3},{3,2},{4,5},{5,4},{6,7},{7,6}} | collective-permute-start | bytes 1769480 | tf_op jit(solution)/shard_map/ppermute | solution.py:450
  27.5 220.0 %collective-permute-start.10 = (bf16[12,192,1536]{2,1,0:T(8,128)(2,1)}, bf16[12,192,1536]{2,1,0:T(8,128)(2,1)}, u32[]{:S(2)}, u32[]{:S(2)}) collective-permute-start(bf16[12,192,1536]{2,1,0:T(8,128)(2,1)} %pad_maximum_fusion.1.refs_2_), channel_id=1, source_target_pairs={{0,2},{1,3},{2,0},{3,1},{4,6},{5,7},{6,4},{7,5}} | collective-permute-start | bytes 21233672 | tf_op jit(solution)/shard_map/ppermute | solution.py:449
  32.4 89.3 %collective-permute-start = (bf16[2048,768]{1,0:T(8,128)(2,1)}, bf16[2048,768]{1,0:T(8,128)(2,1)}, u32[]{:S(2)}, u32[]{:S(2)}) collective-permute-start(bf16[2048,768]{1,0:T(8,128)(2,1)} %fusion.2.own_ref), channel_id=1, source_target_pairs={{0,4},{4,0},{1,5},{5,1},{2,6},{6,2},{3,7},{7,3}} | collective-permute-start | bytes 9437192 | tf_op jit(solution)/shard_map/ppermute | solution.py:455
  37.0 296.9 %collective-permute-start.7 = (bf16[12,192,1536]{2,1,0:T(8,128)(2,1)}, bf16[12,192,1536]{2,1,0:T(8,128)(2,1)}, u32[]{:S(2)}, u32[]{:S(2)}) collective-permute-start(bf16[12,192,1536]{2,1,0:T(8,128)(2,1)} %pad_maximum_fusion.refs_2_), channel_id=1, source_target_pairs={{0,2},{1,3},{2,0},{3,1},{4,6},{5,7},{6,4},{7,5}} | collective-permute-start | bytes 21233672 | tf_op jit(solution)/shard_map/ppermute | solution.py:449
  114.2 132.1 %copy-start = (f32[4096,128]{1,0:T(8,128)}, f32[4096,128]{1,0:T(8,128)S(1)}, u32[]{:S(2)}) copy-start(f32[4096,128]{1,0:T(8,128)S(1)} %get-tuple-element.61.cos_ref) | copy-start | bytes 6291460
  114.2 7.5 collective-permute-start.3
  121.7 212.8 %copy-start.5 = (bf16[2048,768]{1,0:T(8,128)(2,1)S(1)}, bf16[2048,768]{1,0:T(8,128)(2,1)}, u32[]{:S(2)}) copy-start(bf16[2048,768]{1,0:T(8,128)(2,1)} %param.13) | copy-start | bytes 9437188
  246.3 88.2 %collective-permute-start.4 = (bf16[2048,768]{1,0:T(8,128)(2,1)}, bf16[2048,768]{1,0:T(8,128)(2,1)S(1)}, u32[]{:S(2)}, u32[]{:S(2)}) collective-permute-start(bf16[2048,768]{1,0:T(8,128)(2,1)} %get-tuple-element.19), channel_id=1, source_target_pairs={{0,4},{4,0},{1,5},{5,1},{2,6},{6,2},{3,7},{7,3}} | collective-permute-start | bytes 9437192 | tf_op jit(solution)/shard_map/ppermute | solution.py:455
  247.5 182.5 %collective-permute-start.9 = (bf16[12,192,1536]{2,1,0:T(8,128)(2,1)}, bf16[12,192,1536]{2,1,0:T(8,128)(2,1)}, u32[]{:S(2)}, u32[]{:S(2)}) collective-permute-start(bf16[12,192,1536]{2,1,0:T(8,128)(2,1)} %pad_maximum_fusion.1.refs_2_), channel_id=1, source_target_pairs={{0,1},{1,0},{2,3},{3,2},{4,5},{5,4},{6,7},{7,6}} | collective-permute-start | bytes 21233672 | tf_op jit(solution)/shard_map/ppermute | solution.py:450
  247.5 182.5 %collective-permute-start.11 = (bf16[12,192,1536]{2,1,0:T(8,128)(2,1)}, bf16[12,192,1536]{2,1,0:T(8,128)(2,1)}, u32[]{:S(2)}, u32[]{:S(2)}) collective-permute-start(bf16[12,192,1536]{2,1,0:T(8,128)(2,1)} %collective-permute-done.10.refs_4_), channel_id=1, source_target_pairs={{0,1},{1,0},{2,3},{3,2},{4,5},{5,4},{6,7},{7,6}} | collective-permute-start | bytes 21233672 | tf_op jit(solution)/shard_map/ppermute | solution.py:451
  248.0 266.3 %collective-permute-start.6 = (bf16[12,192,1536]{2,1,0:T(8,128)(2,1)}, bf16[12,192,1536]{2,1,0:T(8,128)(2,1)}, u32[]{:S(2)}, u32[]{:S(2)}) collective-permute-start(bf16[12,192,1536]{2,1,0:T(8,128)(2,1)} %pad_maximum_fusion.refs_2_), channel_id=1, source_target_pairs={{0,1},{1,0},{2,3},{3,2},{4,5},{5,4},{6,7},{7,6}} | collective-permute-start | bytes 21233672 | tf_op jit(solution)/shard_map/ppermute | solution.py:450
  333.9 180.5 %collective-permute-start.8 = (bf16[12,192,1536]{2,1,0:T(8,128)(2,1)}, bf16[12,192,1536]{2,1,0:T(8,128)(2,1)}, u32[]{:S(2)}, u32[]{:S(2)}) collective-permute-start(bf16[12,192,1536]{2,1,0:T(8,128)(2,1)} %collective-permute-done.7.refs_4_), channel_id=1, source_target_pairs={{0,1},{1,0},{2,3},{3,2},{4,5},{5,4},{6,7},{7,6}} | collective-permute-start | bytes 21233672 | tf_op jit(solution)/shard_map/ppermute | solution.py:451
  342.8 87.2 %collective-permute-start.5 = (bf16[2048,768]{1,0:T(8,128)(2,1)}, bf16[2048,768]{1,0:T(8,128)(2,1)}, u32[]{:S(2)}, u32[]{:S(2)}) collective-permute-start(bf16[2048,768]{1,0:T(8,128)(2,1)} %multiply_convert_fusion.2.refs_0_), channel_id=1, source_target_pairs={{0,4},{4,0},{1,5},{5,1},{2,6},{6,2},{3,7},{7,3}} | collective-permute-start | bytes 9437192 | tf_op jit(solution)/shard_map/ppermute | solution.py:455
  609.9 65.6 %collective-permute-start.12 = (bf16[2048,768]{1,0:T(8,128)(2,1)}, bf16[2048,768]{1,0:T(8,128)(2,1)S(1)}, u32[]{:S(2)}, u32[]{:S(2)}) collective-permute-start(bf16[2048,768]{1,0:T(8,128)(2,1)} %get-tuple-element.23), channel_id=1, source_target_pairs={{0,4},{4,0},{1,5},{5,1},{2,6},{6,2},{3,7},{7,3}} | collective-permute-start | bytes 9437192 | tf_op jit(solution)/shard_map/ppermute | solution.py:455
  619.3 444.4 %collective-permute-start.23 = (bf16[12,192,1536]{2,1,0:T(8,128)(2,1)}, bf16[12,192,1536]{2,1,0:T(8,128)(2,1)}, u32[]{:S(2)}, u32[]{:S(2)}) collective-permute-start(bf16[12,192,1536]{2,1,0:T(8,128)(2,1)} %pad_maximum_fusion.3.refs_2_), channel_id=1, source_target_pairs={{0,2},{1,3},{2,0},{3,1},{4,6},{5,7},{6,4},{7,5}} | collective-permute-start | bytes 21233672 | tf_op jit(solution)/shard_map/ppermute | solution.py:449
  681.7 258.5 %collective-permute-start.13 = (bf16[2048,768]{1,0:T(8,128)(2,1)}, bf16[2048,768]{1,0:T(8,128)(2,1)}, u32[]{:S(2)}, u32[]{:S(2)}) collective-permute-start(bf16[2048,768]{1,0:T(8,128)(2,1)} %multiply_convert_fusion.1.own_ref), channel_id=1, source_target_pairs={{0,4},{4,0},{1,5},{5,1},{2,6},{6,2},{3,7},{7,3}} | collective-permute-start | bytes 9437192 | tf_op jit(solution)/shard_map/ppermute | solution.py:455
  685.8 254.5 %copy-start.1 = (f32[4096,128]{1,0:T(8,128)S(1)}, f32[4096,128]{1,0:T(8,128)}, u32[]{:S(2)}) copy-start(f32[4096,128]{1,0:T(8,128)} %copy-done) | copy-start | bytes 6291460
  685.8 254.5 %copy-start.3 = (s32[6]{0:T(128)S(1)}, s32[6]{0:T(128)}, u32[]{:S(2)}) copy-start(s32[6]{0:T(128)} %copy-done.2) | copy-start | bytes 76
  689.3 375.0 %collective-permute-start.20 = (bf16[12,192,1536]{2,1,0:T(8,128)(2,1)}, bf16[12,192,1536]{2,1,0:T(8,128)(2,1)}, u32[]{:S(2)}, u32[]{:S(2)}) collective-permute-start(bf16[12,192,1536]{2,1,0:T(8,128)(2,1)} %pad_maximum_fusion.2.refs_2_), channel_id=1, source_target_pairs={{0,2},{1,3},{2,0},{3,1},{4,6},{5,7},{6,4},{7,5}} | collective-permute-start | bytes 21233672 | tf_op jit(solution)/shard_map/ppermute | solution.py:449
  689.9 428.9 %slice-start = ((s8[6291456]{0:T(1024)(128)(4,1)}), s8[4194304]{0:T(1024)(128)(4,1)S(1)}, s32[]{:S(2)}) async-start(s8[6291456]{0:T(1024)(128)(4,1)} %bitcast.79), calls=%async_computation | async-start | bytes 8388608
  689.9 428.8 %slice-start.1 = ((s8[6291456]{0:T(1024)(128)(4,1)}), s8[2097152]{0:T(1024)(128)(4,1)S(1)}, s32[]{:S(2)}) async-start(s8[6291456]{0:T(1024)(128)(4,1)} %bitcast.79), calls=%async_computation.1 | async-start | bytes 4194304
  689.9 242.2 %collective-permute-start.15 = (bf16[192,1536]{1,0:T(8,128)(2,1)S(1)}, bf16[192,1536]{1,0:T(8,128)(2,1)S(1)}, u32[]{:S(2)}, u32[]{:S(2)}) collective-permute-start(bf16[192,1536]{1,0:T(8,128)(2,1)S(1)} %pad_maximum_fusion.5.w0), channel_id=1, source_target_pairs={{0,2},{1,3},{2,0},{3,1},{4,6},{5,7},{6,4},{7,5}} | collective-permute-start | bytes 1769480 | tf_op jit(solution)/shard_map/ppermute | solution.py:449
  691.4 247.2 %collective-permute-start.14 = (bf16[192,1536]{1,0:T(8,128)(2,1)S(1)}, bf16[192,1536]{1,0:T(8,128)(2,1)S(1)}, u32[]{:S(2)}, u32[]{:S(2)}) collective-permute-start(bf16[192,1536]{1,0:T(8,128)(2,1)S(1)} %pad_maximum_fusion.5.w0), channel_id=1, source_target_pairs={{0,1},{1,0},{2,3},{3,2},{4,5},{5,4},{6,7},{7,6}} | collective-permute-start | bytes 1769480 | tf_op jit(solution)/shard_map/ppermute | solution.py:450
  932.2 8.1 collective-permute-start.16
  1063.6 55.1 %collective-permute-start.17 = (bf16[2048,768]{1,0:T(8,128)(2,1)}, bf16[2048,768]{1,0:T(8,128)(2,1)S(1)}, u32[]{:S(2)}, u32[]{:S(2)}) collective-permute-start(bf16[2048,768]{1,0:T(8,128)(2,1)} %get-tuple-element.25), channel_id=1, source_target_pairs={{0,4},{4,0},{1,5},{5,1},{2,6},{6,2},{3,7},{7,3}} | collective-permute-start | bytes 9437192 | tf_op jit(solution)/shard_map/ppermute | solution.py:455
  1063.7 66.9 %collective-permute-start.22 = (bf16[12,192,1536]{2,1,0:T(8,128)(2,1)}, bf16[12,192,1536]{2,1,0:T(8,128)(2,1)}, u32[]{:S(2)}, u32[]{:S(2)}) collective-permute-start(bf16[12,192,1536]{2,1,0:T(8,128)(2,1)} %pad_maximum_fusion.3.refs_2_), channel_id=1, source_target_pairs={{0,1},{1,0},{2,3},{3,2},{4,5},{5,4},{6,7},{7,6}} | collective-permute-start | bytes 21233672 | tf_op jit(solution)/shard_map/ppermute | solution.py:450
  1063.7 66.8 %collective-permute-start.24 = (bf16[12,192,1536]{2,1,0:T(8,128)(2,1)}, bf16[12,192,1536]{2,1,0:T(8,128)(2,1)}, u32[]{:S(2)}, u32[]{:S(2)}) collective-permute-start(bf16[12,192,1536]{2,1,0:T(8,128)(2,1)} %collective-permute-done.23.refs_4_), channel_id=1, source_target_pairs={{0,1},{1,0},{2,3},{3,2},{4,5},{5,4},{6,7},{7,6}} | collective-permute-start | bytes 21233672 | tf_op jit(solution)/shard_map/ppermute | solution.py:451
  1064.2 201.7 %collective-permute-start.19 = (bf16[12,192,1536]{2,1,0:T(8,128)(2,1)}, bf16[12,192,1536]{2,1,0:T(8,128)(2,1)}, u32[]{:S(2)}, u32[]{:S(2)}) collective-permute-start(bf16[12,192,1536]{2,1,0:T(8,128)(2,1)} %pad_maximum_fusion.2.refs_2_), channel_id=1, source_target_pairs={{0,1},{1,0},{2,3},{3,2},{4,5},{5,4},{6,7},{7,6}} | collective-permute-start | bytes 21233672 | tf_op jit(solution)/shard_map/ppermute | solution.py:450
  1064.2 201.7 %collective-permute-start.21 = (bf16[12,192,1536]{2,1,0:T(8,128)(2,1)}, bf16[12,192,1536]{2,1,0:T(8,128)(2,1)}, u32[]{:S(2)}, u32[]{:S(2)}) collective-permute-start(bf16[12,192,1536]{2,1,0:T(8,128)(2,1)} %collective-permute-done.20.refs_4_), channel_id=1, source_target_pairs={{0,1},{1,0},{2,3},{3,2},{4,5},{5,4},{6,7},{7,6}} | collective-permute-start | bytes 21233672 | tf_op jit(solution)/shard_map/ppermute | solution.py:451
  1130.5 51.0 %collective-permute-start.18 = (bf16[2048,768]{1,0:T(8,128)(2,1)S(1)}, bf16[2048,768]{1,0:T(8,128)(2,1)}, u32[]{:S(2)}, u32[]{:S(2)}) collective-permute-start(bf16[2048,768]{1,0:T(8,128)(2,1)S(1)} %multiply_convert_fusion.refs_0_), channel_id=1, source_target_pairs={{0,4},{4,0},{1,5},{5,1},{2,6},{6,2},{3,7},{7,3}} | collective-permute-start | bytes 9437192 | tf_op jit(solution)/shard_map/ppermute | solution.py:455
  1361.1 55.6 %collective-permute-start.25 = (bf16[2048,768]{1,0:T(8,128)(2,1)}, bf16[2048,768]{1,0:T(8,128)(2,1)S(1)}, u32[]{:S(2)}, u32[]{:S(2)}) collective-permute-start(bf16[2048,768]{1,0:T(8,128)(2,1)} %get-tuple-element.27), channel_id=1, source_target_pairs={{0,4},{4,0},{1,5},{5,1},{2,6},{6,2},{3,7},{7,3}} | collective-permute-start | bytes 9437192 | tf_op jit(solution)/shard_map/ppermute | solution.py:455
  (20 other events, 585.8 us)
